TPU v7x, 32 devices: a whole 2x2x4 slice. The times are simulated.
32 devices in a mesh: ang: 8 (over z, x), tile: 4 (over y, core).
Axes of the slice: x: 2, y: 2, z: 4, core: 2. Of those that a mesh axis runs over, the one named last changes fastest.
Arguments:
- sinogram: float32 [2, 64, 2048], P(None, 'ang'), may hold values from -6 to 6
- ray_offsets: int32 [64, 256], P('ang'), may hold values from 0 to 2047
- merge_matrices: float32 [3, 2, 2, 256, 256], replicated, may hold values from -1 to 1.5, as said below
Outputs:
- reconstruction: float32 [2, 2048, 2048], P(None, 'ang')
Inputs may be any that keep to these rules, and one draw needn't show every extreme that they name: merge_matrices[l, b, k] is zero outside the columns b * (96) to b * 96 + 256 / 2 + 31.
All inputs are finite; a program needn't handle non-finite values.
Results may differ from a plain program's by a relative error of at most 0.0003.
Values sent between devices are 32-bit elements; how exact they have to be, the bound alone decides.
No kernel may reach another device: no remote copies, remote signals or barrier semaphores. Data moves between devices by JAX's collectives and lax.ppermute only.
A program may use at most 768 MiB of HBM per device.

v0:
```python
import math

import jax
import jax.numpy as jnp
from jax import lax
from jax.sharding import PartitionSpec as P


def partner_2(array, axis, bit):
    return lax.ppermute(array, axis, [(i, i ^ 1 << bit) for i in range(lax.axis_size(axis))])


def apply_rows(matrix, field):
    return jnp.einsum("rk,skc->src", matrix, field, precision=lax.Precision.HIGHEST)


def smear_rows(sinogram, offsets, first_col, tile_cols):
    slices = sinogram.shape[0]
    angles = sinogram.shape[1]
    bin_count = sinogram.shape[2]
    row_count = offsets.shape[1]
    blocks = angles // 8
    doubled = jnp.concatenate([sinogram, sinogram], axis=2)
    grouped = doubled.reshape(slices, blocks, 8, 2 * bin_count).transpose(1, 2, 0, 3)
    starts = jnp.remainder(offsets + first_col, bin_count)
    grouped_starts = starts.reshape(blocks, 8, row_count)

    def window(angle_rows, start):
        return lax.dynamic_slice_in_dim(angle_rows, start, tile_cols, 1)

    by_rows = jax.vmap(window, in_axes=(None, 0))
    by_angles = jax.vmap(by_rows, in_axes=(0, 0))

    def add_block(running, inputs):
        rows_block, start_block = inputs
        samples = by_angles(rows_block, start_block)
        return (running + jnp.sum(samples, axis=0), None)

    zeros_init = jnp.zeros((row_count, slices, tile_cols), jnp.float32)
    running, _ = lax.scan(add_block, zeros_init, (grouped, grouped_starts))
    return running.transpose(1, 0, 2) / math.sqrt(angles)


def body(sinogram, ray_offsets, merge_matrices):
    row_count = ray_offsets.shape[1]
    margin = row_count // 8
    width = row_count // 2 + margin
    tile_cols = sinogram.shape[2] // lax.axis_size("tile")
    first_col = lax.axis_index("tile") * tile_cols
    partial_value = smear_rows(sinogram, ray_offsets, first_col, tile_cols)
    own_index = lax.axis_index("ang")
    levels = lax.axis_size("ang").bit_length() - 1
    for level_num in range(levels):
        bit_num = levels - 1 - level_num
        own_bit = jnp.right_shift(own_index, bit_num) & 1
        own_matrix = merge_matrices[level_num, own_bit, 0]
        other_matrix = merge_matrices[level_num, own_bit, 1]
        send_start = (1 - own_bit) * (row_count // 2 - margin)
        sent_rows = lax.dynamic_slice_in_dim(partial_value, send_start, width, 1)
        partner = partner_2(sent_rows, "ang", bit_num)
        read_start = own_bit * (row_count // 2 - margin)
        band_matrix = lax.dynamic_slice_in_dim(other_matrix, read_start, width, 1)
        partial_value = apply_rows(own_matrix, partial_value) + apply_rows(band_matrix, partner)
    return lax.all_gather(partial_value, "tile", axis=2, tiled=True)


def solution(mesh):
    placed = (P(None, "ang", None), P("ang", None), P())
    return jax.shard_map(
        body, mesh=mesh, in_specs=placed, out_specs=P(None, "ang", None), check_vma=False
    )
```

profile of v0, /device:TPU:0, one launch (start us, length us, event | category | flops | bytes accessed | tf_op | source)
XLA Modules:
  0.0 1160.0 jit_solution(3746597719928638852)
XLA Ops:
  6.5 0.0 copy-start
  6.5 0.0 all-gather.2.cloned.1.call-start
  6.5 0.9 fusion.24
  7.4 1.1 pad_maximum_fusion
  8.5 8.9 copy.11
  17.3 796.7 %gather_fusion = f32[2048,2,512]{1,0,2:T(8,128)} fusion(f32[8,2,4096]{1,0,2:T(8,128)} %bitcast.69, s32[2048]{0:T(1024)S(1)} %bitcast.70), kind=kCustom, calls=%fused_computation | custom fusion | bytes 16801792 | tf_op jit(solution)/shard_map/while/body/eval_jaxpr/vmap(vmap())/gather | solution.py:29
  814.0 178.7 %reduce_sum.10 = f32[256,2,512]{1,0,2:T(8,128)} reduce(f32[8,256,2,512]{2,1,0,3:T(8,128)} %bitcast.4, f32[]{:T(128)} %constant.137.clone.1), dimensions={0}, to_apply=%region_0.1 | reduce | flops 1835008 | bytes 9437188 | tf_op jit(solution)/shard_map/while/body/eval_jaxpr/reduce_sum | solution.py:37
  992.7 37.8 %copy.12 = f32[256,2,512]{2,0,1:T(8,128)} copy(f32[256,2,512]{1,0,2:T(8,128)} %reduce_sum.10) | data formatting | bytes 2097152 | tf_op jit(solution)/shard_map/while/body/eval_jaxpr/reduce_sum | solution.py:37
  1030.5 2.3 broadcast_multiply_fusion
  1032.8 2.0 dynamic-slice_bitcast_fusion.2
  1034.9 2.5 collective-permute-start
  1037.4 0.0 copy-done
  1037.4 2.3 fusion.5
  1039.7 26.4 %collective-permute-done = f32[2,160,512]{2,1,0:T(8,128)} collective-permute-done((f32[2,160,512]{2,1,0:T(8,128)}, f32[2,160,512]{2,1,0:T(8,128)}, u32[]{:S(2)}, u32[]{:S(2)}) %collective-permute-start) | collective-permute-done | bytes 655392 | tf_op jit(solution)/shard_map/ppermute | solution.py:10
  1066.1 2.1 convolution_add_fusion.2
  1068.3 0.0 copy-start.1
  1068.3 1.0 copy-done.1
  1069.2 0.9 dynamic-slice_bitcast_fusion.1
  1070.1 0.7 collective-permute-start.1
  1070.8 2.3 fusion.3
  1073.2 12.9 %collective-permute-done.1 = f32[2,160,512]{2,1,0:T(8,128)} collective-permute-done((f32[2,160,512]{2,1,0:T(8,128)}, f32[2,160,512]{2,1,0:T(8,128)}, u32[]{:S(2)}, u32[]{:S(2)}) %collective-permute-start.1) | collective-permute-done | bytes 655392 | tf_op jit(solution)/shard_map/ppermute | solution.py:10
  1086.1 2.1 convolution_add_fusion.1
  1088.2 0.0 copy-start.2
  1088.2 1.0 copy-done.2
  1089.2 0.9 dynamic-slice_bitcast_fusion
  1090.1 4.5 collective-permute-start.2
  1094.6 3.0 fusion.1
  1097.6 11.4 collective-permute-done.2
  1109.1 4.0 fusion
  1113.0 0.0 all-gather.2.cloned.1.call-update
  1113.1 34.8 %all-gather.2.cloned.1.call-done = f32[2,256,2048]{1,2,0:T(8,128)} async-done(((f32[2,256,512]{1,2,0:T(8,128)}), f32[2,256,2048]{1,2,0:T(8,128)}) %all-gather.2.cloned.1.call-update) | async-done | bytes 4194320 | tf_op jit(solution)/shard_map/all_gather | solution.py:64
  1147.9 5.3 copy.17
  (1 shorter events, 0.0 us)
Async XLA Ops:
  6.5 1030.9 %copy-start = (f32[3,2,2,256,256]{4,3,2,1,0:T(8,128)S(1)}, f32[3,2,2,256,256]{4,3,2,1,0:T(8,128)}, u32[]{:S(2)}) copy-start(f32[3,2,2,256,256]{4,3,2,1,0:T(8,128)} %param.5) | copy-start | bytes 9437188
  6.5 1141.3 %all-gather.2.cloned.1.call-start = ((), (), s32[]{:S(2)}) async-start(), calls=%async_computation | async-start | bytes 5242880 | tf_op jit(solution)/shard_map/all_gather | solution.py:64
  1034.9 31.3 %collective-permute-start = (f32[2,160,512]{2,1,0:T(8,128)}, f32[2,160,512]{2,1,0:T(8,128)}, u32[]{:S(2)}, u32[]{:S(2)}) collective-permute-start(f32[2,160,512]{2,1,0:T(8,128)} %dynamic-slice_bitcast_fusion.2), channel_id=1, source_target_pairs={{0,16},{4,20},{8,24},{12,28},{16,0},{20,4},{24,8},{28,12},{1,17},{... | collective-permute-start | bytes 1966088 | tf_op jit(solution)/shard_map/ppermute | solution.py:10
  1068.3 1.0 copy-start.1
  1070.1 16.0 %collective-permute-start.1 = (f32[2,160,512]{2,1,0:T(8,128)}, f32[2,160,512]{2,1,0:T(8,128)}, u32[]{:S(2)}, u32[]{:S(2)}) collective-permute-start(f32[2,160,512]{2,1,0:T(8,128)} %dynamic-slice_bitcast_fusion.1), channel_id=1, source_target_pairs={{0,8},{4,12},{8,0},{12,4},{16,24},{20,28},{24,16},{28,20},{1,9},{5... | collective-permute-start | bytes 1966088 | tf_op jit(solution)/shard_map/ppermute | solution.py:10
  1088.2 1.0 copy-start.2
  1090.1 19.0 %collective-permute-start.2 = (f32[2,160,512]{2,1,0:T(8,128)}, f32[2,160,512]{2,1,0:T(8,128)}, u32[]{:S(2)}, u32[]{:S(2)}) collective-permute-start(f32[2,160,512]{2,1,0:T(8,128)} %dynamic-slice_bitcast_fusion), channel_id=1, source_target_pairs={{0,4},{4,0},{8,12},{12,8},{16,20},{20,16},{24,28},{28,24},{1,5},{5... | collective-permute-start | bytes 1966088 | tf_op jit(solution)/shard_map/ppermute | solution.py:10
Sparse Core Ops, SparseCore 0:
  1113.2 34.6 all-gather.1
where the time goes:
time: 1160 us
  local copies, waits for them, and re-layouts  854 us (74%)
  other arithmetic  183 us (16%)
  waiting for transfers between devices  85.6 us (7%)
  matrix products  15.9 us (1%)
  between operations  13.5 us (1%)
    gather x1, local copies, waits for them, and re-layouts, window(): return lax.dynamic_slice_in_dim(angle_rows, start, tile_cols, 1)  797 us
    reduce_sum x1, other arithmetic, add_block(): return (running + jnp.sum(samples, axis=0), None)  179 us
    ppermute x3, waiting for transfers between devices, partner_2(): lax.ppermute(array, axis, [(i, i ^ 1 << bit) for i in range(lax.axis_size...  50.8 us
    reduce_sum x1, local copies, waits for them, and re-layouts, add_block(): return (running + jnp.sum(samples, axis=0), None)  37.8 us
    all_gather x1, waiting for transfers between devices, body(): return lax.all_gather(partial_value, 'tile', axis=2, tiled=True)  34.8 us
  transfers between devices with their start and end apart: 4, of which 4 were waited for; matrix products, arithmetic and copies ran while one was open for 1% of the time, Pallas kernels for 0%

commit v1 on v0

v1 whole, which is shorter than its diff:
```python
import functools
import math

import jax
import jax.numpy as jnp
from jax import lax
from jax.experimental import pallas as pl
from jax.experimental.pallas import tpu as pltpu
from jax.sharding import PartitionSpec as P

LANES = 128
SUBLANES = 8


def packed_rows(sinogram, ray_offsets):
    slices, angles, bin_count = sinogram.shape
    rows = ray_offsets.shape[1]
    half = angles // 2
    run = slices * bin_count // LANES
    fields = sinogram.reshape(slices, 2, half, bin_count // run, run).transpose(1, 2, 4, 0, 3)
    fields = fields.reshape(2, half * run, LANES)
    words = ray_offsets.astype(jnp.float32).reshape(2, half, SUBLANES, rows // SUBLANES)
    words = words.transpose(0, 2, 1, 3).reshape(2, SUBLANES, -1)
    words = jnp.pad(words, ((0, 0), (0, 0), (0, LANES - words.shape[2])))
    return jnp.concatenate([fields, words], axis=1)


def split(value):
    high = value.astype(jnp.bfloat16)
    return high, (value - high.astype(jnp.float32)).astype(jnp.bfloat16)


def dot(left, right):
    return jnp.dot(left, right, preferred_element_type=jnp.float32)


class Smear:
    def __init__(self, half, slices, run, unroll, band, band_blocks, lines, staged, words, shift, tables):
        self.half, self.slices, self.run, self.unroll = half, slices, run, unroll
        self.band, self.band_blocks = band, band_blocks
        self.lines, self.staged, self.words, self.shift, self.tables = lines, staged, words, shift, tables
        self.lane_blocks = LANES // slices
        self.table_rows = (self.lane_blocks + 1) * run
        self.angles = 2 * half

    def put(self, place, part, source):
        size = self.half * self.run
        high, low = split(source[:size, :])
        where = pl.ds(pl.multiple_of((place * 2 + part) * size, size), size)
        self.lines[where, :LANES] = high
        self.lines[where, LANES:] = low
        where = pl.multiple_of((place * 2 + part) * SUBLANES, SUBLANES)
        self.staged[pl.ds(where, SUBLANES), :] = source[size:, :].astype(jnp.int32)

    def shift_matrices(self):
        line = lax.broadcasted_iota(jnp.int32, (2 * LANES, LANES), 0)
        lane = lax.broadcasted_iota(jnp.int32, (2 * LANES, LANES), 1)
        same = ((line // self.lane_blocks) % self.slices) == lane // self.lane_blocks
        distance = jnp.where(same, (line - lane) & (self.lane_blocks - 1), -1)
        for m in range(self.lane_blocks):
            self.shift[:, m * LANES : (m + 1) * LANES] = jnp.where(distance == m, 1.0, 0.0).astype(jnp.bfloat16)

    def build(self, place, table, first, count):
        size = self.angles * self.run
        lines = self.lines[place * size : (place + 1) * size, :]
        for m in range(count):
            columns = pl.ds(pl.multiple_of((first + m) * (2 * LANES), 2 * LANES), 2 * LANES)
            shifted = dot(lines, self.shift[:, columns])
            for a in range(self.angles):
                for n in range(2):
                    block = shifted[a * self.run : (a + 1) * self.run, n * LANES : (n + 1) * LANES]
                    start = pl.multiple_of((first + m) * (2 * self.run), SUBLANES)
                    table[pl.ds(start + (a * self.table_rows + n * self.run), self.run), :] = block

    def close(self, table):
        for a in range(self.angles):
            start = a * self.table_rows
            last = start + self.lane_blocks * self.run
            table[last : last + self.run, :] = table[start : start + self.run, :]

    def gather(self, place, table, step, partial, pitch, first, last):
        word_row = place * (2 * SUBLANES) + self.band + step
        first_sample = (place * self.band_blocks + step) * self.unroll
        vectors = self.run // SUBLANES
        for u in range(first, last):
            sums = [None] * vectors
            for a in range(self.angles):
                offset = self.words[word_row + (a // self.half) * SUBLANES, (a % self.half) * self.unroll + u]
                for n in range(vectors):
                    piece = table[pl.ds(offset + (a * self.table_rows + n * SUBLANES), SUBLANES), :]
                    sums[n] = piece if sums[n] is None else sums[n] + piece
            for n in range(vectors):
                start = first_sample + (u + n * SUBLANES * pitch)
                partial[pl.ds(start, SUBLANES, stride=pitch), :] = sums[n]

    def run_groups(self, count, partial, pitch):
        pairs = self.lane_blocks // 2
        share = -(-pairs // self.band_blocks)

        def first_step(step, carry):
            self.build(0, self.tables[0], jnp.minimum(step * share, pairs - share), share)
            return carry

        lax.fori_loop(0, self.band_blocks, first_step, 0)
        self.close(self.tables[0])
        for place in range(count):
            now, later = self.tables[place % 2], self.tables[(place + 1) % 2]

            def merged_step(step, carry):
                self.gather(place, now, step, partial, pitch, 0, self.unroll)
                return carry

            lax.fori_loop(0, self.band_blocks, merged_step, 0)
            if place + 1 < count:
                self.build(place + 1, later, 0, pairs)
                self.close(later)


def matrices_kernel(levels, width, angles, place_ref, all_ref, high_ref, low_ref, pair_ref, sems):
    copies = []
    for level in range(levels):
        own_bit = (place_ref[2] >> (levels - 1 - level)) & 1
        copies.append(pltpu.make_async_copy(all_ref.at[level, own_bit], pair_ref.at[level], sems.at[level]))
        copies[-1].start()
    rows = pair_ref.shape[2]
    scale = 1.0 / math.sqrt(angles)
    product = None
    for level in reversed(range(levels)):
        copies[level].wait()
        pair = [pair_ref[level, n] for n in range(2)]
        if level == 0:
            upper = place_ref[1] > 0
            pair = [jnp.where(upper, m[:, rows - width :], m[:, :width]) * scale for m in pair]
        if product is None:
            product = pair
            continue
        pair = [split(m) for m in pair]
        left = [split(m) for m in product]
        product = [
            dot(high, other_low) + dot(low, other_high) + dot(high, other_high)
            for other_high, other_low in pair
            for high, low in left
        ]
    high_ref[...], low_ref[...] = split(jnp.concatenate(product, axis=1))


def early_kernel(smear_sizes, pitch, place_ref, own_ref, neighbour_ref,
                 early_ref, lines_ref, staged_ref, words_ref, shift_ref, table_a, table_b, sem):
    half, slices, run, unroll, band_blocks = smear_sizes
    smear = Smear(half, slices, run, unroll, place_ref[1], band_blocks, lines_ref, staged_ref, words_ref, shift_ref, (table_a, table_b))
    for part in range(2):
        smear.put(0, part, own_ref.at[part])
        smear.put(1, part, neighbour_ref.at[part])
    copy = pltpu.make_async_copy(staged_ref, words_ref, sem)
    copy.start()
    smear.shift_matrices()
    copy.wait()
    smear.run_groups(2, early_ref, pitch)


def image_kernel(smear_sizes, size, width, early_pitch, pitch, turn_pitch, place_ref, *refs):
    early_ref, high_ref, low_ref = refs[size - 2 : size + 1]
    (out_ref, lines_ref, staged_ref, words_ref, shift_ref, table_a, table_b, partial_ref, turned_ref, sem) = refs[size + 1 :]
    half, slices, run, unroll, band_blocks = smear_sizes
    core = place_ref[0]
    smear = Smear(half, slices, run, unroll, place_ref[1], band_blocks, lines_ref, staged_ref, words_ref, shift_ref, (table_a, table_b))
    lane_blocks = smear.lane_blocks
    rows = out_ref.shape[1]
    for pair in range(size // 2 - 1):
        for group in range(2):
            smear.put(2 * pair + group, core, refs[2 * pair].at[group])
            smear.put(2 * pair + group, 1 - core, refs[2 * pair + 1].at[group])
    copy = pltpu.make_async_copy(staged_ref, words_ref, sem)
    copy.start()
    smear.shift_matrices()
    copy.wait()
    smear.run_groups(size - 2, partial_ref, pitch)

    def column_block(index):
        return jnp.concatenate(
            [
                early_ref[pl.ds(pl.multiple_of(index * early_pitch, 8), 2 * width), :],
                partial_ref[pl.ds(pl.multiple_of(index * pitch, 8), (size - 2) * width), :],
            ],
            axis=0,
        )

    def multiply_block(step, carry):
        field = jnp.concatenate([column_block(2 * step), column_block(2 * step + 1)], axis=1)
        field_high, field_low = split(field)
        left_high = high_ref[...]
        value = dot(left_high, field_low) + dot(low_ref[...], field_high)
        value = value + dot(left_high, field_high)
        for n in range(2):
            turned = value[:, n * LANES : (n + 1) * LANES].T
            for r in range(0, rows, LANES):
                part = min(LANES, rows - r)
                start = (r // LANES) * (LANES * turn_pitch) + 2 * step + n
                turned_ref[pl.ds(start, LANES, stride=turn_pitch), :part] = turned[:, r : r + part]
        return carry

    lax.fori_loop(0, run // 2, multiply_block, 0)

    per = LANES // run

    def turn_block(step, carry):
        for s in range(slices):
            for r in range(0, rows, LANES):
                part = min(LANES, rows - r)
                base = (r // LANES) * (LANES * turn_pitch)
                pieces = [
                    turned_ref[pl.ds(base + (s * lane_blocks + step * per + n) * turn_pitch, run), :part]
                    for n in range(per)
                ]
                columns = pl.ds(pl.multiple_of(step * LANES, LANES), LANES)
                out_ref[s, r : r + part, columns] = jnp.concatenate(pieces, axis=0).T
        return carry

    lax.fori_loop(0, lane_blocks // per, turn_block, 0)


def body(sinogram, ray_offsets, merge_matrices):
    slices, angles, bin_count = sinogram.shape
    rows = ray_offsets.shape[1]
    margin = rows // SUBLANES
    width = rows // 2 + margin
    size = lax.axis_size("ang")
    tiles = lax.axis_size("tile")
    core = lax.axis_index("tile") & 1
    own_index = lax.axis_index("ang")
    top_bit = jnp.right_shift(own_index, size.bit_length() - 2) & 1
    band_block = top_bit * (SUBLANES // 2 - 1)
    run = slices * bin_count // LANES
    lane_blocks = LANES // slices

    def other_core(array):
        return lax.ppermute(array, "tile", [(i, i ^ 1) for i in range(tiles)])

    def from_group(array, k):
        return lax.ppermute(array, "ang", [(i, i ^ k) for i in range(size)])

    own = packed_rows(sinogram, ray_offsets)
    neighbour = from_group(own, 1)
    mine = jnp.stack([own[core], neighbour[core]])
    place = jnp.stack([core, band_block, own_index]).astype(jnp.int32)

    def spread(count):
        return count + (8 - count) % 32

    early_pitch = spread(2 * width)
    pitch = spread((size - 2) * width)
    turn_pitch = run + 1
    in_vmem = pl.BlockSpec(memory_space=pltpu.VMEM)
    in_smem = pl.BlockSpec(memory_space=pltpu.SMEM)
    smear_sizes = (angles // 2, slices, run, margin, width // margin)

    def smear_scratch(count):
        return [
            pltpu.VMEM((count * angles * run, 2 * LANES), jnp.bfloat16),
            pltpu.VMEM((count * 2 * SUBLANES, LANES), jnp.int32),
            pltpu.SMEM((count * 2 * SUBLANES, LANES), jnp.int32),
            pltpu.VMEM((2 * LANES, lane_blocks * LANES), jnp.bfloat16),
            pltpu.VMEM((angles * (lane_blocks + 1) * run, LANES), jnp.float32),
            pltpu.VMEM((angles * (lane_blocks + 1) * run, LANES), jnp.float32),
        ]

    levels = merge_matrices.shape[0]
    high, low = pl.pallas_call(
        functools.partial(matrices_kernel, levels, width, angles),
        name="matrices",
        out_shape=(jax.ShapeDtypeStruct((rows, size * width), jnp.bfloat16),) * 2,
        in_specs=[in_smem, pl.BlockSpec(memory_space=pl.ANY)],
        out_specs=(in_vmem,) * 2,
        scratch_shapes=[
            pltpu.VMEM((levels,) + merge_matrices.shape[2:], jnp.float32),
            pltpu.SemaphoreType.DMA((levels,)),
        ],
        cost_estimate=pl.CostEstimate(flops=5 * 10**8, bytes_accessed=10**6, transcendentals=0),
        compiler_params=pltpu.CompilerParams(vmem_limit_bytes=32 * 2**20),
    )(place, merge_matrices)
    early = pl.pallas_call(
        functools.partial(early_kernel, smear_sizes, early_pitch),
        name="early",
        out_shape=jax.ShapeDtypeStruct((run * early_pitch, LANES), jnp.float32),
        in_specs=[in_smem] + [in_vmem] * 2,
        out_specs=in_vmem,
        scratch_shapes=smear_scratch(2) + [pltpu.SemaphoreType.DMA],
        cost_estimate=pl.CostEstimate(flops=2 * 10**9, bytes_accessed=10**7, transcendentals=0),
        compiler_params=pltpu.CompilerParams(vmem_limit_bytes=36 * 2**20),
    )(place, own, neighbour)
    mine, high = lax.optimization_barrier((mine, high))
    arrived = [from_group(mine, 2 * pair) for pair in range(1, size // 2)]
    arrived[-1], early = lax.optimization_barrier((arrived[-1], early))
    operands = []
    for array in arrived:
        operands += [array, other_core(array)]
    return pl.pallas_call(
        functools.partial(image_kernel, smear_sizes, size, width, early_pitch, pitch, turn_pitch),
        name="image",
        out_shape=jax.ShapeDtypeStruct((slices, rows, bin_count), jnp.float32),
        in_specs=[in_smem] + [in_vmem] * (size - 2) + [in_vmem] * 3,
        out_specs=in_vmem,
        scratch_shapes=smear_scratch(size - 2)
        + [
            pltpu.VMEM((run * pitch, LANES), jnp.float32),
            pltpu.VMEM((-(-rows // LANES) * LANES * turn_pitch, LANES), jnp.float32),
            pltpu.SemaphoreType.DMA,
        ],
        cost_estimate=pl.CostEstimate(flops=10**10, bytes_accessed=10**7, transcendentals=0),
        compiler_params=pltpu.CompilerParams(vmem_limit_bytes=52 * 2**20),
    )(place, *operands, early, high, low)


def solution(mesh):
    placed = (P(None, "ang", None), P("ang", None), P())
    return jax.shard_map(
        body, mesh=mesh, in_specs=placed, out_specs=P(None, "ang", None), check_vma=False
    )
```

time: 1160 us -> 67.8 us (0.06)
  local copies, waits for them, and re-layouts: 854 us -> 5.92 us
  other arithmetic: 183 us -> 0.79 us
  waiting for transfers between devices: 85.6 us -> 1.29 us
  Pallas kernels: 0 us -> 51.3 us
  matrix products: 15.9 us -> 0 us
  between operations: 13.5 us -> 0.28 us
    gather x1 -> x0, local copies, waits for them, and re-layouts: 797 us -> none  [window(): return lax.dynamic_slice_in_dim(angle_rows, start, tile_cols, 1)]
    reduce_sum x1 -> x0, other arithmetic: 179 us -> none  [add_block(): return (running + jnp.sum(samples, axis=0), None)]
    pallas_call x0 -> x3, Pallas kernels: none -> 51.3 us  [the longest x1 40.1 us: body(): pl.pallas_call(functools.partial(image_kernel, smear_sizes, size, width,...]
    ppermute x3 -> x7, waiting for transfers between devices: 50.8 us -> 1.29 us  [the longest x3 1.28 us: other_core(): return lax.ppermute(array, 'tile', [(i, i ^ 1) for i in range(tiles)])]
    reduce_sum x1 -> x0, local copies, waits for them, and re-layouts: 37.8 us -> none  [add_block(): return (running + jnp.sum(samples, axis=0), None)]
    all_gather x1 -> x0, waiting for transfers between devices: 34.8 us -> none  [body(): return lax.all_gather(partial_value, 'tile', axis=2, tiled=True)]
    dot_general x6 -> x0, matrix products: 15.9 us -> none  [apply_rows(): jnp.einsum('rk,skc->src', matrix, field, precision=lax.Precision.HIGHEST)]
  transfers between devices with their start and end apart: 4 -> 7, of which waited for: 4 -> 3; matrix products, arithmetic and copies ran while one was open for 1% -> 0% of each run, Pallas kernels for 0% -> 17%
where the time goes in v1:
time: 67.8 us; the launch traced here: 67.6 us
  Pallas kernels  51.3 us (76%)
  starting transfers between devices  8.06 us (12%)
  local copies, waits for them, and re-layouts  5.92 us (9%)
  waiting for transfers between devices  1.29 us (2%)
  other arithmetic  0.79 us (1%)
    pallas_call x1, Pallas kernels, body(): pl.pallas_call(functools.partial(image_kernel, smear_sizes, size, width,...  40.1 us
    pallas_call x1, Pallas kernels, body(): pl.pallas_call(functools.partial(early_kernel, smear_sizes, early_pitch),...  8.58 us
    ppermute x4, starting transfers between devices, from_group(): return lax.ppermute(array, 'ang', [(i, i ^ k) for i in range(size)])  7.48 us
    unnamed x7, local copies, waits for them, and re-layouts  4.25 us
    pallas_call x1, Pallas kernels, body(): pl.pallas_call(functools.partial(matrices_kernel, levels, width, angles),...  2.61 us
  transfers between devices with their start and end apart: 7, of which 3 were waited for; matrix products, arithmetic and copies ran while one was open for 0% of the time, Pallas kernels for 17%

profile of v1, /device:TPU:0, one launch (start us, length us, event | category | flops | bytes accessed | tf_op | source)
XLA Modules:
  0.0 67.6 jit_solution(15346731186567193134)
XLA Ops:
  0.0 0.7 %convert_element_type.3 = f32[8,256]{1,0:T(8,128)S(1)} convert(s32[8,256]{1,0:T(8,128)} %param.4) | non-fusion elementwise | flops 2048 | bytes 16384 | tf_op jit(solution)/shard_map/convert_element_type | solution.py:22
  0.7 0.1 reshape.14
  0.8 0.1 reshape.15
  0.9 1.1 %reshape.12 = f32[2,2,4,64,32]{4,3,2,1,0:T(8,128)S(1)} reshape(f32[2,8,2048]{2,1,0:T(8,128)} %param.3) | data formatting | bytes 262144 | tf_op jit(solution)/shard_map/reshape | solution.py:20
  2.0 0.2 copy.6
  2.2 0.2 reshape.13
  2.4 3.0 %collective-permute-start = (f32[2,136,128]{2,1,0:T(8,128)S(1)}, f32[2,136,128]{2,1,0:T(8,128)S(1)}, u32[]{:S(2)}, u32[]{:S(2)}) collective-permute-start(f32[2,136,128]{2,1,0:T(8,128)S(1)} %constant_dynamic-update-slice_fusion.own_ref), channel_id=1, source_target_pairs={{0,4},{4,0},{8,12},{12,8},{16,20},{20,16},{24,28},{28,24},{1,5},{5... | collective-permute-start | bytes 417800 | tf_op jit(solution)/shard_map/ppermute | solution.py:240
  5.4 0.1 pad_add_fusion.place_ref
  5.5 0.0 copy-start
  5.5 1.9 %copy-done = f32[3,2,2,256,256]{4,3,2,1,0:T(8,128)S(1)} copy-done((f32[3,2,2,256,256]{4,3,2,1,0:T(8,128)S(1)}, f32[3,2,2,256,256]{4,3,2,1,0:T(8,128)}, u32[]{:S(2)}) %copy-start) | copy-done | bytes 3145752
  7.4 2.6 %matrices.1 = (bf16[256,1280]{1,0:T(8,128)(2,1)S(1)}, bf16[256,1280]{1,0:T(8,128)(2,1)S(1)}) custom-call(s32[3]{0:T(128)S(1)} %pad_add_fusion.place_ref, f32[3,2,2,256,256]{4,3,2,1,0:T(8,128)S(1)} %copy-done), custom_call_target="tpu_custom_call" | custom-call | flops 500000000 | bytes 1000000 | tf_op jit(solution)/shard_map/matrices/pallas_call | solution.py:268
  10.0 0.0 copy-start.1
  10.0 0.0 collective-permute-done.neighbour_ref
  10.1 3.7 %collective-permute-start.5 = (f32[2,136,128]{2,1,0:T(8,128)S(1)}, f32[2,136,128]{2,1,0:T(8,128)S(1)}, u32[]{:S(2)}, u32[]{:S(2)}) collective-permute-start(f32[2,136,128]{2,1,0:T(8,128)S(1)} %pad_maximum_fusion), channel_id=1, source_target_pairs={{0,24},{4,28},{8,16},{12,20},{16,8},{20,12},{24,0},{28,4},{1,25},{... | collective-permute-start | bytes 417800 | tf_op jit(solution)/shard_map/ppermute | solution.py:240
  13.8 0.0 collective-permute-start.3
  13.8 0.8 %collective-permute-start.1 = (f32[2,136,128]{2,1,0:T(8,128)S(1)}, f32[2,136,128]{2,1,0:T(8,128)S(1)}, u32[]{:S(2)}, u32[]{:S(2)}) collective-permute-start(f32[2,136,128]{2,1,0:T(8,128)S(1)} %pad_maximum_fusion), channel_id=1, source_target_pairs={{0,8},{4,12},{8,0},{12,4},{16,24},{20,28},{24,16},{28,20},{1,9},{5... | collective-permute-start | bytes 417800 | tf_op jit(solution)/shard_map/ppermute | solution.py:240
  14.5 8.6 %early.1.refs_6_ = f32[10496,128]{1,0:T(8,128)S(1)} custom-call(s32[3]{0:T(128)S(1)} %pad_add_fusion.place_ref, f32[2,136,128]{2,1,0:T(8,128)S(1)} %constant_dynamic-update-slice_fusion.own_ref, f32[2,136,128]{2,1,0:T(8,128)S(1)} %collective-permute-done.neighbour_ref), custom_call_target="tpu_custom_call" | custom-call | flops 2000000000 | bytes 10000000 | tf_op jit(solution)/shard_map/early/pallas_call | solution.py:281
  23.1 0.0 copy-done.1
  23.1 0.0 copy-start.2
  23.1 2.3 %copy-done.2 = f32[10496,128]{1,0:T(8,128)} copy-done((f32[10496,128]{1,0:T(8,128)}, f32[10496,128]{1,0:T(8,128)S(1)}, u32[]{:S(2)}) %copy-start.2) | copy-done | bytes 5373976
  25.5 0.0 collective-permute-done.5.refs_4_
  25.5 0.0 collective-permute-done.3.refs_2_
  25.5 0.0 collective-permute-start.4
  25.5 0.0 collective-permute-done.1.refs_0_
  25.5 0.5 collective-permute-start.2
  26.0 0.1 collective-permute-start.6
  26.1 0.8 %collective-permute-done.4.refs_3_ = f32[2,136,128]{2,1,0:T(8,128)S(1)} collective-permute-done((f32[2,136,128]{2,1,0:T(8,128)S(1)}, f32[2,136,128]{2,1,0:T(8,128)S(1)}, u32[]{:S(2)}, u32[]{:S(2)}) %collective-permute-start.4) | collective-permute-done | bytes 139296 | tf_op jit(solution)/shard_map/ppermute | solution.py:237
  26.9 0.2 collective-permute-done.2.refs_1_
  27.1 0.3 collective-permute-done.6.refs_5_
  27.4 40.1 %image.1 = f32[2,256,2048]{2,1,0:T(8,128)} custom-call(s32[3]{0:T(128)S(1)} %pad_add_fusion.place_ref, f32[2,136,128]{2,1,0:T(8,128)S(1)} %collective-permute-done.1.refs_0_, f32[2,136,128]{2,1,0:T(8,128)S(1)} %collective-permute-done.2.refs_1_, f32[2,136,128]{2,1,0:T(8,128)S(1)} %collective-permute-done.3.refs_2_, ...), custom_call_target="tpu_custom_call" | custom-call | flops 10000000000 | bytes 10000000 | tf_op jit(solution)/shard_map/image/pallas_call | solution.py:297
  (6 shorter events, 0.1 us)
Async XLA Ops:
  2.4 7.7 %collective-permute-start = (f32[2,136,128]{2,1,0:T(8,128)S(1)}, f32[2,136,128]{2,1,0:T(8,128)S(1)}, u32[]{:S(2)}, u32[]{:S(2)}) collective-permute-start(f32[2,136,128]{2,1,0:T(8,128)S(1)} %constant_dynamic-update-slice_fusion.own_ref), channel_id=1, source_target_pairs={{0,4},{4,0},{8,12},{12,8},{16,20},{20,16},{24,28},{28,24},{1,5},{5... | collective-permute-start | bytes 417800 | tf_op jit(solution)/shard_map/ppermute | solution.py:240
  5.5 1.9 %copy-start = (f32[3,2,2,256,256]{4,3,2,1,0:T(8,128)S(1)}, f32[3,2,2,256,256]{4,3,2,1,0:T(8,128)}, u32[]{:S(2)}) copy-start(f32[3,2,2,256,256]{4,3,2,1,0:T(8,128)} %all_ref.1) | copy-start | bytes 9437188
  10.0 13.1 %copy-start.1 = (bf16[256,1280]{1,0:T(8,128)(2,1)}, bf16[256,1280]{1,0:T(8,128)(2,1)S(1)}, u32[]{:S(2)}) copy-start(bf16[256,1280]{1,0:T(8,128)(2,1)S(1)} %get-tuple-element.16.refs_8_) | copy-start | bytes 1966084
  10.1 15.4 %collective-permute-start.5 = (f32[2,136,128]{2,1,0:T(8,128)S(1)}, f32[2,136,128]{2,1,0:T(8,128)S(1)}, u32[]{:S(2)}, u32[]{:S(2)}) collective-permute-start(f32[2,136,128]{2,1,0:T(8,128)S(1)} %pad_maximum_fusion), channel_id=1, source_target_pairs={{0,24},{4,28},{8,16},{12,20},{16,8},{20,12},{24,0},{28,4},{1,25},{... | collective-permute-start | bytes 417800 | tf_op jit(solution)/shard_map/ppermute | solution.py:240
  13.8 11.7 %collective-permute-start.3 = (f32[2,136,128]{2,1,0:T(8,128)S(1)}, f32[2,136,128]{2,1,0:T(8,128)S(1)}, u32[]{:S(2)}, u32[]{:S(2)}) collective-permute-start(f32[2,136,128]{2,1,0:T(8,128)S(1)} %pad_maximum_fusion), channel_id=1, source_target_pairs={{0,16},{4,20},{8,24},{12,28},{16,0},{20,4},{24,8},{28,12},{1,17},{... | collective-permute-start | bytes 417800 | tf_op jit(solution)/shard_map/ppermute | solution.py:240
  13.8 11.7 %collective-permute-start.1 = (f32[2,136,128]{2,1,0:T(8,128)S(1)}, f32[2,136,128]{2,1,0:T(8,128)S(1)}, u32[]{:S(2)}, u32[]{:S(2)}) collective-permute-start(f32[2,136,128]{2,1,0:T(8,128)S(1)} %pad_maximum_fusion), channel_id=1, source_target_pairs={{0,8},{4,12},{8,0},{12,4},{16,24},{20,28},{24,16},{28,20},{1,9},{5... | collective-permute-start | bytes 417800 | tf_op jit(solution)/shard_map/ppermute | solution.py:240
  23.1 2.3 %copy-start.2 = (f32[10496,128]{1,0:T(8,128)}, f32[10496,128]{1,0:T(8,128)S(1)}, u32[]{:S(2)}) copy-start(f32[10496,128]{1,0:T(8,128)S(1)} %early.1.refs_6_) | copy-start | bytes 16121860
  25.5 1.4 %collective-permute-start.4 = (f32[2,136,128]{2,1,0:T(8,128)S(1)}, f32[2,136,128]{2,1,0:T(8,128)S(1)}, u32[]{:S(2)}, u32[]{:S(2)}) collective-permute-start(f32[2,136,128]{2,1,0:T(8,128)S(1)} %collective-permute-done.3.refs_2_), channel_id=1, source_target_pairs={{0,1},{1,0},{2,3},{3,2},{4,5},{5,4},{6,7},{7,6},{8,9},{9,8},{10,11... | collective-permute-start | bytes 417800 | tf_op jit(solution)/shard_map/ppermute | solution.py:237
  25.5 1.5 %collective-permute-start.2 = (f32[2,136,128]{2,1,0:T(8,128)S(1)}, f32[2,136,128]{2,1,0:T(8,128)S(1)}, u32[]{:S(2)}, u32[]{:S(2)}) collective-permute-start(f32[2,136,128]{2,1,0:T(8,128)S(1)} %collective-permute-done.1.refs_0_), channel_id=1, source_target_pairs={{0,1},{1,0},{2,3},{3,2},{4,5},{5,4},{6,7},{7,6},{8,9},{9,8},{10,11... | collective-permute-start | bytes 417800 | tf_op jit(solution)/shard_map/ppermute | solution.py:237
  26.0 1.4 %collective-permute-start.6 = (f32[2,136,128]{2,1,0:T(8,128)S(1)}, f32[2,136,128]{2,1,0:T(8,128)S(1)}, u32[]{:S(2)}, u32[]{:S(2)}) collective-permute-start(f32[2,136,128]{2,1,0:T(8,128)S(1)} %collective-permute-done.5.refs_4_), channel_id=1, source_target_pairs={{0,1},{1,0},{2,3},{3,2},{4,5},{5,4},{6,7},{7,6},{8,9},{9,8},{10,11... | collective-permute-start | bytes 417800 | tf_op jit(solution)/shard_map/ppermute | solution.py:237

commit v2 on v1

--- a/solution.py
+++ b/solution.py
@@ -35,9 +35,10 @@
 
 
 class Smear:
-    def __init__(self, half, slices, run, unroll, band, band_blocks, lines, staged, words, shift, tables):
+    def __init__(self, half, slices, run, unroll, core, band, band_blocks, lines, staged, words, shift, tables):
         self.half, self.slices, self.run, self.unroll = half, slices, run, unroll
         self.band, self.band_blocks = band, band_blocks
+        self.skip_rows = core * (run // 2)
         self.lines, self.staged, self.words, self.shift, self.tables = lines, staged, words, shift, tables
         self.lane_blocks = LANES // slices
         self.table_rows = (self.lane_blocks + 1) * run
@@ -50,7 +51,7 @@
         self.lines[where, :LANES] = high
         self.lines[where, LANES:] = low
         where = pl.multiple_of((place * 2 + part) * SUBLANES, SUBLANES)
-        self.staged[pl.ds(where, SUBLANES), :] = source[size:, :].astype(jnp.int32)
+        self.staged[pl.ds(where, SUBLANES), :] = source[size:, :].astype(jnp.int32) + self.skip_rows
 
     def shift_matrices(self):
         line = lax.broadcasted_iota(jnp.int32, (2 * LANES, LANES), 0)
@@ -78,10 +79,10 @@
             last = start + self.lane_blocks * self.run
             table[last : last + self.run, :] = table[start : start + self.run, :]
 
-    def gather(self, place, table, step, partial, pitch, first, last):
+    def gather(self, place, table, step, partial, pitch, first, last, skip):
         word_row = place * (2 * SUBLANES) + self.band + step
-        first_sample = (place * self.band_blocks + step) * self.unroll
-        vectors = self.run // SUBLANES
+        first_sample = ((place + skip) * self.band_blocks + step) * self.unroll
+        vectors = self.run // (2 * SUBLANES)
         for u in range(first, last):
             sums = [None] * vectors
             for a in range(self.angles):
@@ -93,21 +94,21 @@
                 start = first_sample + (u + n * SUBLANES * pitch)
                 partial[pl.ds(start, SUBLANES, stride=pitch), :] = sums[n]
 
-    def run_groups(self, count, partial, pitch):
+    def run_groups(self, count, partial, pitch, skip=0):
         pairs = self.lane_blocks // 2
         share = -(-pairs // self.band_blocks)
 
         def first_step(step, carry):
-            self.build(0, self.tables[0], jnp.minimum(step * share, pairs - share), share)
+            self.build(0, self.tables, jnp.minimum(step * share, pairs - share), share)
             return carry
 
         lax.fori_loop(0, self.band_blocks, first_step, 0)
-        self.close(self.tables[0])
+        self.close(self.tables)
         for place in range(count):
-            now, later = self.tables[place % 2], self.tables[(place + 1) % 2]
+            now = later = self.tables
 
             def merged_step(step, carry):
-                self.gather(place, now, step, partial, pitch, 0, self.unroll)
+                self.gather(place, now, step, partial, pitch, 0, self.unroll, skip)
                 return carry
 
             lax.fori_loop(0, self.band_blocks, merged_step, 0)
@@ -145,9 +146,9 @@
 
 
 def early_kernel(smear_sizes, pitch, place_ref, own_ref, neighbour_ref,
-                 early_ref, lines_ref, staged_ref, words_ref, shift_ref, table_a, table_b, sem):
+                 early_ref, lines_ref, staged_ref, words_ref, shift_ref, table_a, sem):
     half, slices, run, unroll, band_blocks = smear_sizes
-    smear = Smear(half, slices, run, unroll, place_ref[1], band_blocks, lines_ref, staged_ref, words_ref, shift_ref, (table_a, table_b))
+    smear = Smear(half, slices, run, unroll, place_ref[0], place_ref[1], band_blocks, lines_ref, staged_ref, words_ref, shift_ref, table_a)
     for part in range(2):
         smear.put(0, part, own_ref.at[part])
         smear.put(1, part, neighbour_ref.at[part])
@@ -160,12 +161,11 @@
 
 def image_kernel(smear_sizes, size, width, early_pitch, pitch, turn_pitch, place_ref, *refs):
     early_ref, high_ref, low_ref = refs[size - 2 : size + 1]
-    (out_ref, lines_ref, staged_ref, words_ref, shift_ref, table_a, table_b, partial_ref, turned_ref, sem) = refs[size + 1 :]
+    (out_ref, lines_ref, staged_ref, words_ref, shift_ref, table_a, partial_ref, sem) = refs[size + 1 :]
     half, slices, run, unroll, band_blocks = smear_sizes
     core = place_ref[0]
-    smear = Smear(half, slices, run, unroll, place_ref[1], band_blocks, lines_ref, staged_ref, words_ref, shift_ref, (table_a, table_b))
-    lane_blocks = smear.lane_blocks
-    rows = out_ref.shape[1]
+    smear = Smear(half, slices, run, unroll, place_ref[0], place_ref[1], band_blocks, lines_ref, staged_ref, words_ref, shift_ref, table_a)
+    rows = high_ref.shape[0]
     for pair in range(size // 2 - 1):
         for group in range(2):
             smear.put(2 * pair + group, core, refs[2 * pair].at[group])
@@ -174,16 +174,16 @@
     copy.start()
     smear.shift_matrices()
     copy.wait()
-    smear.run_groups(size - 2, partial_ref, pitch)
+    def copy_early(index, carry):
+        where = pl.ds(pl.multiple_of(index * pitch, 8), 2 * width)
+        partial_ref[where, :] = early_ref[pl.ds(pl.multiple_of(index * early_pitch, 8), 2 * width), :]
+        return carry
+
+    lax.fori_loop(0, run // 2, copy_early, 0)
+    smear.run_groups(size - 2, partial_ref, pitch, 2)
 
     def column_block(index):
-        return jnp.concatenate(
-            [
-                early_ref[pl.ds(pl.multiple_of(index * early_pitch, 8), 2 * width), :],
-                partial_ref[pl.ds(pl.multiple_of(index * pitch, 8), (size - 2) * width), :],
-            ],
-            axis=0,
-        )
+        return partial_ref[pl.ds(pl.multiple_of(index * pitch, 8), size * width), :]
 
     def multiply_block(step, carry):
         field = jnp.concatenate([column_block(2 * step), column_block(2 * step + 1)], axis=1)
@@ -196,27 +196,30 @@
             for r in range(0, rows, LANES):
                 part = min(LANES, rows - r)
                 start = (r // LANES) * (LANES * turn_pitch) + 2 * step + n
-                turned_ref[pl.ds(start, LANES, stride=turn_pitch), :part] = turned[:, r : r + part]
+                out_ref[pl.ds(start, LANES, stride=turn_pitch), :part] = turned[:, r : r + part]
         return carry
 
-    lax.fori_loop(0, run // 2, multiply_block, 0)
-
+    lax.fori_loop(0, run // 4, multiply_block, 0, unroll=2)
+
+
+def finish_kernel(slices, run, turn_pitch, place_ref, own_ref, other_ref, out_ref):
+    swap = place_ref[0] == 0
+    lane_blocks = LANES // slices
     per = LANES // run
+    part = out_ref.shape[1]
 
     def turn_block(step, carry):
         for s in range(slices):
-            for r in range(0, rows, LANES):
-                part = min(LANES, rows - r)
-                base = (r // LANES) * (LANES * turn_pitch)
-                pieces = [
-                    turned_ref[pl.ds(base + (s * lane_blocks + step * per + n) * turn_pitch, run), :part]
-                    for n in range(per)
-                ]
-                columns = pl.ds(pl.multiple_of(step * LANES, LANES), LANES)
-                out_ref[s, r : r + part, columns] = jnp.concatenate(pieces, axis=0).T
+            pieces = []
+            for n in range(per):
+                rows = pl.ds((s * lane_blocks + step * per + n) * turn_pitch, run // 2)
+                own, other = own_ref[rows, :], other_ref[rows, :]
+                pieces += [jnp.where(swap, own, other), jnp.where(swap, other, own)]
+            columns = pl.ds(pl.multiple_of(step * LANES, LANES), LANES)
+            out_ref[s, :, columns] = jnp.concatenate(pieces, axis=0).T[:part]
         return carry
 
-    lax.fori_loop(0, lane_blocks // per, turn_block, 0)
+    lax.fori_loop(0, lane_blocks // per, turn_block, 0, unroll=2)
 
 
 def body(sinogram, ray_offsets, merge_matrices):
@@ -248,8 +251,10 @@
         return count + (8 - count) % 32
 
     early_pitch = spread(2 * width)
-    pitch = spread((size - 2) * width)
-    turn_pitch = run + 1
+    pitch = spread(size * width)
+    turn_pitch = run // 2 + 1
+    turn_blocks = -(-rows // LANES)
+    turned_rows = LANES * turn_pitch
     in_vmem = pl.BlockSpec(memory_space=pltpu.VMEM)
     in_smem = pl.BlockSpec(memory_space=pltpu.SMEM)
     smear_sizes = (angles // 2, slices, run, margin, width // margin)
@@ -261,7 +266,6 @@
             pltpu.SMEM((count * 2 * SUBLANES, LANES), jnp.int32),
             pltpu.VMEM((2 * LANES, lane_blocks * LANES), jnp.bfloat16),
             pltpu.VMEM((angles * (lane_blocks + 1) * run, LANES), jnp.float32),
-            pltpu.VMEM((angles * (lane_blocks + 1) * run, LANES), jnp.float32),
         ]
 
     levels = merge_matrices.shape[0]
@@ -269,7 +273,7 @@
         functools.partial(matrices_kernel, levels, width, angles),
         name="matrices",
         out_shape=(jax.ShapeDtypeStruct((rows, size * width), jnp.bfloat16),) * 2,
-        in_specs=[in_smem, pl.BlockSpec(memory_space=pl.ANY)],
+        in_specs=[in_smem, pl.BlockSpec(memory_space=pltpu.HBM)],
         out_specs=(in_vmem,) * 2,
         scratch_shapes=[
             pltpu.VMEM((levels,) + merge_matrices.shape[2:], jnp.float32),
@@ -281,7 +285,7 @@
     early = pl.pallas_call(
         functools.partial(early_kernel, smear_sizes, early_pitch),
         name="early",
-        out_shape=jax.ShapeDtypeStruct((run * early_pitch, LANES), jnp.float32),
+        out_shape=jax.ShapeDtypeStruct((run // 2 * early_pitch, LANES), jnp.float32),
         in_specs=[in_smem] + [in_vmem] * 2,
         out_specs=in_vmem,
         scratch_shapes=smear_scratch(2) + [pltpu.SemaphoreType.DMA],
@@ -294,21 +298,32 @@
     operands = []
     for array in arrived:
         operands += [array, other_core(array)]
-    return pl.pallas_call(
+    turned = pl.pallas_call(
         functools.partial(image_kernel, smear_sizes, size, width, early_pitch, pitch, turn_pitch),
         name="image",
-        out_shape=jax.ShapeDtypeStruct((slices, rows, bin_count), jnp.float32),
+        out_shape=jax.ShapeDtypeStruct((turn_blocks * turned_rows, LANES), jnp.float32),
         in_specs=[in_smem] + [in_vmem] * (size - 2) + [in_vmem] * 3,
         out_specs=in_vmem,
         scratch_shapes=smear_scratch(size - 2)
         + [
-            pltpu.VMEM((run * pitch, LANES), jnp.float32),
-            pltpu.VMEM((-(-rows // LANES) * LANES * turn_pitch, LANES), jnp.float32),
+            pltpu.VMEM((run // 2 * pitch, LANES), jnp.float32),
             pltpu.SemaphoreType.DMA,
         ],
         cost_estimate=pl.CostEstimate(flops=10**10, bytes_accessed=10**7, transcendentals=0),
-        compiler_params=pltpu.CompilerParams(vmem_limit_bytes=52 * 2**20),
+        compiler_params=pltpu.CompilerParams(vmem_limit_bytes=40 * 2**20),
     )(place, *operands, early, high, low)
+    rows_spec = pl.BlockSpec((turned_rows, LANES), lambda i: (i, 0))
+    block_rows = min(rows, LANES)
+    return pl.pallas_call(
+        functools.partial(finish_kernel, slices, run, turn_pitch),
+        name="finish",
+        out_shape=jax.ShapeDtypeStruct((slices, rows, bin_count), jnp.float32),
+        grid=(turn_blocks,),
+        in_specs=[in_smem, rows_spec, rows_spec],
+        out_specs=pl.BlockSpec((slices, block_rows, bin_count), lambda i: (0, i, 0)),
+        cost_estimate=pl.CostEstimate(flops=10**8, bytes_accessed=10**7, transcendentals=0),
+        compiler_params=pltpu.CompilerParams(vmem_limit_bytes=24 * 2**20),
+    )(place, turned, other_core(turned))
 
 
 def solution(mesh):

time: 67.8 us -> 59.4 us (0.88)
  Pallas kernels: 51.3 us -> 37.7 us
  waiting for transfers between devices: 1.29 us -> 8.77 us
  local copies, waits for them, and re-layouts: 5.92 us -> 3.57 us
    pallas_call x1, Pallas kernels: 40.1 us -> 23.6 us  [body(): pl.pallas_call(functools.partial(image_kernel, smear_sizes, size, width,...]
    ppermute x3 -> x4, waiting for transfers between devices: 1.28 us -> 5.5 us  [other_core(): return lax.ppermute(array, 'tile', [(i, i ^ 1) for i in range(tiles)])]
    pallas_call x0 -> x1, Pallas kernels: none -> 4.07 us  [body(): pl.pallas_call(functools.partial(finish_kernel, slices, run, turn_pitch),...]
    ppermute x4, waiting for transfers between devices: 0.01 us -> 3.27 us  [from_group(): return lax.ppermute(array, 'ang', [(i, i ^ k) for i in range(size)])]
    unnamed x7 -> x3, local copies, waits for them, and re-layouts: 4.25 us -> 1.9 us
    pallas_call x1, Pallas kernels: 8.58 us -> 7.44 us  [body(): pl.pallas_call(functools.partial(early_kernel, smear_sizes, early_pitch),...]
  transfers between devices with their start and end apart: 7 -> 8, of which waited for: 3 -> 5; matrix products, arithmetic and copies ran while one was open for 0% -> 0% of each run, Pallas kernels for 17% -> 17%
where the time goes in v2:
time: 59.4 us; the launch traced here: 59.2 us
  Pallas kernels  37.7 us (63%)
  waiting for transfers between devices  8.77 us (15%)
  starting transfers between devices  8.26 us (14%)
  local copies, waits for them, and re-layouts  3.57 us (6%)
  other arithmetic  0.79 us (1%)
    pallas_call x1, Pallas kernels, body(): pl.pallas_call(functools.partial(image_kernel, smear_sizes, size, width,...  23.6 us
    ppermute x4, starting transfers between devices, from_group(): return lax.ppermute(array, 'ang', [(i, i ^ k) for i in range(size)])  7.48 us
    pallas_call x1, Pallas kernels, body(): pl.pallas_call(functools.partial(early_kernel, smear_sizes, early_pitch),...  7.44 us
    ppermute x4, waiting for transfers between devices, other_core(): return lax.ppermute(array, 'tile', [(i, i ^ 1) for i in range(tiles)])  5.5 us
    pallas_call x1, Pallas kernels, body(): pl.pallas_call(functools.partial(finish_kernel, slices, run, turn_pitch),...  4.07 us
    ppermute x4, waiting for transfers between devices, from_group(): return lax.ppermute(array, 'ang', [(i, i ^ k) for i in range(size)])  3.27 us
    pallas_call x1, Pallas kernels, body(): pl.pallas_call(functools.partial(matrices_kernel, levels, width, angles),...  2.61 us
    unnamed x3, local copies, waits for them, and re-layouts  1.9 us
  transfers between devices with their start and end apart: 8, of which 5 were waited for; matrix products, arithmetic and copies ran while one was open for 0% of the time, Pallas kernels for 17%

profile of v2, /device:TPU:0, one launch (start us, length us, event | category | flops | bytes accessed | tf_op | source)
XLA Modules:
  0.0 59.2 jit_solution(9242659803044122140)
XLA Ops:
  0.0 0.7 %convert_element_type.3 = f32[8,256]{1,0:T(8,128)S(1)} convert(s32[8,256]{1,0:T(8,128)} %param.4) | non-fusion elementwise | flops 2048 | bytes 16384 | tf_op jit(solution)/shard_map/convert_element_type | solution.py:22
  0.7 0.1 reshape.14
  0.8 0.1 reshape.15
  0.9 1.1 %reshape.12 = f32[2,2,4,64,32]{4,3,2,1,0:T(8,128)S(1)} reshape(f32[2,8,2048]{2,1,0:T(8,128)} %param.3) | data formatting | bytes 262144 | tf_op jit(solution)/shard_map/reshape | solution.py:20
  2.0 0.2 copy.6
  2.2 0.2 reshape.13
  2.4 3.0 %collective-permute-start = (f32[2,136,128]{2,1,0:T(8,128)S(1)}, f32[2,136,128]{2,1,0:T(8,128)S(1)}, u32[]{:S(2)}, u32[]{:S(2)}) collective-permute-start(f32[2,136,128]{2,1,0:T(8,128)S(1)} %constant_dynamic-update-slice_fusion.own_ref), channel_id=1, source_target_pairs={{0,4},{4,0},{8,12},{12,8},{16,20},{20,16},{24,28},{28,24},{1,5},{5... | collective-permute-start | bytes 417800 | tf_op jit(solution)/shard_map/ppermute | solution.py:243
  5.4 0.1 pad_add_fusion.place_ref
  5.5 0.0 copy-start
  5.5 1.9 %copy-done = f32[3,2,2,256,256]{4,3,2,1,0:T(8,128)S(1)} copy-done((f32[3,2,2,256,256]{4,3,2,1,0:T(8,128)S(1)}, f32[3,2,2,256,256]{4,3,2,1,0:T(8,128)}, u32[]{:S(2)}) %copy-start) | copy-done | bytes 3145752
  7.4 2.6 %matrices.1 = (bf16[256,1280]{1,0:T(8,128)(2,1)S(1)}, bf16[256,1280]{1,0:T(8,128)(2,1)S(1)}) custom-call(s32[3]{0:T(128)S(1)} %pad_add_fusion.place_ref, f32[3,2,2,256,256]{4,3,2,1,0:T(8,128)S(1)} %copy-done), custom_call_target="tpu_custom_call" | custom-call | flops 500000000 | bytes 1000000 | tf_op jit(solution)/shard_map/matrices/pallas_call | solution.py:272
  10.0 0.0 collective-permute-done.neighbour_ref
  10.1 3.7 %collective-permute-start.5 = (f32[2,136,128]{2,1,0:T(8,128)S(1)}, f32[2,136,128]{2,1,0:T(8,128)S(1)}, u32[]{:S(2)}, u32[]{:S(2)}) collective-permute-start(f32[2,136,128]{2,1,0:T(8,128)S(1)} %pad_maximum_fusion), channel_id=1, source_target_pairs={{0,24},{4,28},{8,16},{12,20},{16,8},{20,12},{24,0},{28,4},{1,25},{... | collective-permute-start | bytes 417800 | tf_op jit(solution)/shard_map/ppermute | solution.py:243
  13.7 0.0 collective-permute-start.3
  13.7 0.8 %collective-permute-start.1 = (f32[2,136,128]{2,1,0:T(8,128)S(1)}, f32[2,136,128]{2,1,0:T(8,128)S(1)}, u32[]{:S(2)}, u32[]{:S(2)}) collective-permute-start(f32[2,136,128]{2,1,0:T(8,128)S(1)} %pad_maximum_fusion), channel_id=1, source_target_pairs={{0,8},{4,12},{8,0},{12,4},{16,24},{20,28},{24,16},{28,20},{1,9},{5... | collective-permute-start | bytes 417800 | tf_op jit(solution)/shard_map/ppermute | solution.py:243
  14.5 7.4 %early.1.refs_6_ = f32[5248,128]{1,0:T(8,128)S(1)} custom-call(s32[3]{0:T(128)S(1)} %pad_add_fusion.place_ref, f32[2,136,128]{2,1,0:T(8,128)S(1)} %constant_dynamic-update-slice_fusion.own_ref, f32[2,136,128]{2,1,0:T(8,128)S(1)} %collective-permute-done.neighbour_ref), custom_call_target="tpu_custom_call" | custom-call | flops 2000000000 | bytes 10000000 | tf_op jit(solution)/shard_map/early/pallas_call | solution.py:285
  22.0 0.0 collective-permute-done.5.refs_4_
  22.0 3.3 %collective-permute-done.3.refs_2_ = f32[2,136,128]{2,1,0:T(8,128)S(1)} collective-permute-done((f32[2,136,128]{2,1,0:T(8,128)S(1)}, f32[2,136,128]{2,1,0:T(8,128)S(1)}, u32[]{:S(2)}, u32[]{:S(2)}) %collective-permute-start.3) | collective-permute-done | bytes 139296 | tf_op jit(solution)/shard_map/ppermute | solution.py:243
  25.2 0.0 collective-permute-start.4
  25.2 0.0 collective-permute-done.1.refs_0_
  25.2 0.5 collective-permute-start.2
  25.8 0.0 collective-permute-start.6
  25.8 0.8 %collective-permute-done.4.refs_3_ = f32[2,136,128]{2,1,0:T(8,128)S(1)} collective-permute-done((f32[2,136,128]{2,1,0:T(8,128)S(1)}, f32[2,136,128]{2,1,0:T(8,128)S(1)}, u32[]{:S(2)}, u32[]{:S(2)}) %collective-permute-start.4) | collective-permute-done | bytes 139296 | tf_op jit(solution)/shard_map/ppermute | solution.py:240
  26.6 0.2 collective-permute-done.2.refs_1_
  26.8 0.3 collective-permute-done.6.refs_5_
  27.1 23.6 %image.1.own_ref = f32[4352,128]{1,0:T(8,128)S(1)} custom-call(s32[3]{0:T(128)S(1)} %pad_add_fusion.place_ref, f32[2,136,128]{2,1,0:T(8,128)S(1)} %collective-permute-done.1.refs_0_, f32[2,136,128]{2,1,0:T(8,128)S(1)} %collective-permute-done.2.refs_1_, f32[2,136,128]{2,1,0:T(8,128)S(1)} %collective-permute-done.3.refs_2_, ...), custom_call_target="tpu_custom_call" | custom-call | flops 10000000000 | bytes 10000000 | tf_op jit(solution)/shard_map/image/pallas_call | solution.py:301
  50.7 0.3 collective-permute-start.7
  51.0 4.1 %collective-permute-done.7.other_ref = f32[4352,128]{1,0:T(8,128)S(1)} collective-permute-done((f32[4352,128]{1,0:T(8,128)S(1)}, f32[4352,128]{1,0:T(8,128)S(1)}, u32[]{:S(2)}, u32[]{:S(2)}) %collective-permute-start.7) | collective-permute-done | bytes 2228256 | tf_op jit(solution)/shard_map/ppermute | solution.py:240
  55.2 4.1 %finish.1 = f32[2,256,2048]{2,1,0:T(8,128)} custom-call(s32[3]{0:T(128)S(1)} %pad_add_fusion.place_ref, f32[4352,128]{1,0:T(8,128)S(1)} %image.1.own_ref, f32[4352,128]{1,0:T(8,128)S(1)} %collective-permute-done.7.other_ref), custom_call_target="tpu_custom_call" | custom-call | flops 100000000 | bytes 10000000 | tf_op jit(solution)/shard_map/finish/pallas_call | solution.py:317
  (6 shorter events, 0.1 us)
Async XLA Ops:
  2.4 7.6 %collective-permute-start = (f32[2,136,128]{2,1,0:T(8,128)S(1)}, f32[2,136,128]{2,1,0:T(8,128)S(1)}, u32[]{:S(2)}, u32[]{:S(2)}) collective-permute-start(f32[2,136,128]{2,1,0:T(8,128)S(1)} %constant_dynamic-update-slice_fusion.own_ref), channel_id=1, source_target_pairs={{0,4},{4,0},{8,12},{12,8},{16,20},{20,16},{24,28},{28,24},{1,5},{5... | collective-permute-start | bytes 417800 | tf_op jit(solution)/shard_map/ppermute | solution.py:243
  5.5 1.9 %copy-start = (f32[3,2,2,256,256]{4,3,2,1,0:T(8,128)S(1)}, f32[3,2,2,256,256]{4,3,2,1,0:T(8,128)}, u32[]{:S(2)}) copy-start(f32[3,2,2,256,256]{4,3,2,1,0:T(8,128)} %all_ref.1) | copy-start | bytes 9437188
  10.1 11.9 %collective-permute-start.5 = (f32[2,136,128]{2,1,0:T(8,128)S(1)}, f32[2,136,128]{2,1,0:T(8,128)S(1)}, u32[]{:S(2)}, u32[]{:S(2)}) collective-permute-start(f32[2,136,128]{2,1,0:T(8,128)S(1)} %pad_maximum_fusion), channel_id=1, source_target_pairs={{0,24},{4,28},{8,16},{12,20},{16,8},{20,12},{24,0},{28,4},{1,25},{... | collective-permute-start | bytes 417800 | tf_op jit(solution)/shard_map/ppermute | solution.py:243
  13.7 11.5 %collective-permute-start.3 = (f32[2,136,128]{2,1,0:T(8,128)S(1)}, f32[2,136,128]{2,1,0:T(8,128)S(1)}, u32[]{:S(2)}, u32[]{:S(2)}) collective-permute-start(f32[2,136,128]{2,1,0:T(8,128)S(1)} %pad_maximum_fusion), channel_id=1, source_target_pairs={{0,16},{4,20},{8,24},{12,28},{16,0},{20,4},{24,8},{28,12},{1,17},{... | collective-permute-start | bytes 417800 | tf_op jit(solution)/shard_map/ppermute | solution.py:243
  13.7 11.5 %collective-permute-start.1 = (f32[2,136,128]{2,1,0:T(8,128)S(1)}, f32[2,136,128]{2,1,0:T(8,128)S(1)}, u32[]{:S(2)}, u32[]{:S(2)}) collective-permute-start(f32[2,136,128]{2,1,0:T(8,128)S(1)} %pad_maximum_fusion), channel_id=1, source_target_pairs={{0,8},{4,12},{8,0},{12,4},{16,24},{20,28},{24,16},{28,20},{1,9},{5... | collective-permute-start | bytes 417800 | tf_op jit(solution)/shard_map/ppermute | solution.py:243
  25.2 1.4 %collective-permute-start.4 = (f32[2,136,128]{2,1,0:T(8,128)S(1)}, f32[2,136,128]{2,1,0:T(8,128)S(1)}, u32[]{:S(2)}, u32[]{:S(2)}) collective-permute-start(f32[2,136,128]{2,1,0:T(8,128)S(1)} %collective-permute-done.3.refs_2_), channel_id=1, source_target_pairs={{0,1},{1,0},{2,3},{3,2},{4,5},{5,4},{6,7},{7,6},{8,9},{9,8},{10,11... | collective-permute-start | bytes 417800 | tf_op jit(solution)/shard_map/ppermute | solution.py:240
  25.2 1.6 %collective-permute-start.2 = (f32[2,136,128]{2,1,0:T(8,128)S(1)}, f32[2,136,128]{2,1,0:T(8,128)S(1)}, u32[]{:S(2)}, u32[]{:S(2)}) collective-permute-start(f32[2,136,128]{2,1,0:T(8,128)S(1)} %collective-permute-done.1.refs_0_), channel_id=1, source_target_pairs={{0,1},{1,0},{2,3},{3,2},{4,5},{5,4},{6,7},{7,6},{8,9},{9,8},{10,11... | collective-permute-start | bytes 417800 | tf_op jit(solution)/shard_map/ppermute | solution.py:240
  25.8 1.4 %collective-permute-start.6 = (f32[2,136,128]{2,1,0:T(8,128)S(1)}, f32[2,136,128]{2,1,0:T(8,128)S(1)}, u32[]{:S(2)}, u32[]{:S(2)}) collective-permute-start(f32[2,136,128]{2,1,0:T(8,128)S(1)} %collective-permute-done.5.refs_4_), channel_id=1, source_target_pairs={{0,1},{1,0},{2,3},{3,2},{4,5},{5,4},{6,7},{7,6},{8,9},{9,8},{10,11... | collective-permute-start | bytes 417800 | tf_op jit(solution)/shard_map/ppermute | solution.py:240
  50.7 4.4 %collective-permute-start.7 = (f32[4352,128]{1,0:T(8,128)S(1)}, f32[4352,128]{1,0:T(8,128)S(1)}, u32[]{:S(2)}, u32[]{:S(2)}) collective-permute-start(f32[4352,128]{1,0:T(8,128)S(1)} %image.1.own_ref), channel_id=1, source_target_pairs={{0,1},{1,0},{2,3},{3,2},{4,5},{5,4},{6,7},{7,6},{8,9},{9,8},{10,11... | collective-permute-start | bytes 6684680 | tf_op jit(solution)/shard_map/ppermute | solution.py:240

commit v3 on v2

--- a/solution.py
+++ b/solution.py
@@ -96,13 +96,7 @@
 
     def run_groups(self, count, partial, pitch, skip=0):
         pairs = self.lane_blocks // 2
-        share = -(-pairs // self.band_blocks)
-
-        def first_step(step, carry):
-            self.build(0, self.tables, jnp.minimum(step * share, pairs - share), share)
-            return carry
-
-        lax.fori_loop(0, self.band_blocks, first_step, 0)
+        self.build(0, self.tables, 0, pairs)
         self.close(self.tables)
         for place in range(count):
             now = later = self.tables
@@ -146,7 +140,7 @@
 
 
 def early_kernel(smear_sizes, pitch, place_ref, own_ref, neighbour_ref,
-                 early_ref, lines_ref, staged_ref, words_ref, shift_ref, table_a, sem):
+                 early_ref, shift_ref, lines_ref, staged_ref, words_ref, table_a, sem):
     half, slices, run, unroll, band_blocks = smear_sizes
     smear = Smear(half, slices, run, unroll, place_ref[0], place_ref[1], band_blocks, lines_ref, staged_ref, words_ref, shift_ref, table_a)
     for part in range(2):
@@ -160,8 +154,8 @@
 
 
 def image_kernel(smear_sizes, size, width, early_pitch, pitch, turn_pitch, place_ref, *refs):
-    early_ref, high_ref, low_ref = refs[size - 2 : size + 1]
-    (out_ref, lines_ref, staged_ref, words_ref, shift_ref, table_a, partial_ref, sem) = refs[size + 1 :]
+    early_ref, shift_ref, high_ref, low_ref = refs[size - 2 : size + 2]
+    (out_ref, lines_ref, staged_ref, words_ref, table_a, partial_ref, sem) = refs[size + 2 :]
     half, slices, run, unroll, band_blocks = smear_sizes
     core = place_ref[0]
     smear = Smear(half, slices, run, unroll, place_ref[0], place_ref[1], band_blocks, lines_ref, staged_ref, words_ref, shift_ref, table_a)
@@ -172,18 +166,17 @@
             smear.put(2 * pair + group, 1 - core, refs[2 * pair + 1].at[group])
     copy = pltpu.make_async_copy(staged_ref, words_ref, sem)
     copy.start()
-    smear.shift_matrices()
     copy.wait()
     def copy_early(index, carry):
-        where = pl.ds(pl.multiple_of(index * pitch, 8), 2 * width)
-        partial_ref[where, :] = early_ref[pl.ds(pl.multiple_of(index * early_pitch, 8), 2 * width), :]
+        where = pl.ds(index * pitch, 2 * width)
+        partial_ref[where, :] = early_ref[pl.ds(index * early_pitch, 2 * width), :]
         return carry
 
     lax.fori_loop(0, run // 2, copy_early, 0)
     smear.run_groups(size - 2, partial_ref, pitch, 2)
 
     def column_block(index):
-        return partial_ref[pl.ds(pl.multiple_of(index * pitch, 8), size * width), :]
+        return partial_ref[pl.ds(index * pitch, size * width), :]
 
     def multiply_block(step, carry):
         field = jnp.concatenate([column_block(2 * step), column_block(2 * step + 1)], axis=1)
@@ -199,7 +192,7 @@
                 out_ref[pl.ds(start, LANES, stride=turn_pitch), :part] = turned[:, r : r + part]
         return carry
 
-    lax.fori_loop(0, run // 4, multiply_block, 0, unroll=2)
+    lax.fori_loop(0, run // 4, multiply_block, 0, unroll=4)
 
 
 def finish_kernel(slices, run, turn_pitch, place_ref, own_ref, other_ref, out_ref):
@@ -219,7 +212,7 @@
             out_ref[s, :, columns] = jnp.concatenate(pieces, axis=0).T[:part]
         return carry
 
-    lax.fori_loop(0, lane_blocks // per, turn_block, 0, unroll=2)
+    lax.fori_loop(0, lane_blocks // per, turn_block, 0, unroll=4)
 
 
 def body(sinogram, ray_offsets, merge_matrices):
@@ -248,7 +241,7 @@
     place = jnp.stack([core, band_block, own_index]).astype(jnp.int32)
 
     def spread(count):
-        return count + (8 - count) % 32
+        return count + (12 - count) % 32
 
     early_pitch = spread(2 * width)
     pitch = spread(size * width)
@@ -264,7 +257,6 @@
             pltpu.VMEM((count * angles * run, 2 * LANES), jnp.bfloat16),
             pltpu.VMEM((count * 2 * SUBLANES, LANES), jnp.int32),
             pltpu.SMEM((count * 2 * SUBLANES, LANES), jnp.int32),
-            pltpu.VMEM((2 * LANES, lane_blocks * LANES), jnp.bfloat16),
             pltpu.VMEM((angles * (lane_blocks + 1) * run, LANES), jnp.float32),
         ]
 
@@ -282,19 +274,21 @@
         cost_estimate=pl.CostEstimate(flops=5 * 10**8, bytes_accessed=10**6, transcendentals=0),
         compiler_params=pltpu.CompilerParams(vmem_limit_bytes=32 * 2**20),
     )(place, merge_matrices)
-    early = pl.pallas_call(
+    early, shift = pl.pallas_call(
         functools.partial(early_kernel, smear_sizes, early_pitch),
         name="early",
-        out_shape=jax.ShapeDtypeStruct((run // 2 * early_pitch, LANES), jnp.float32),
+        out_shape=(
+            jax.ShapeDtypeStruct((run // 2 * early_pitch, LANES), jnp.float32),
+            jax.ShapeDtypeStruct((2 * LANES, lane_blocks * LANES), jnp.bfloat16),
+        ),
         in_specs=[in_smem] + [in_vmem] * 2,
-        out_specs=in_vmem,
+        out_specs=(in_vmem,) * 2,
         scratch_shapes=smear_scratch(2) + [pltpu.SemaphoreType.DMA],
         cost_estimate=pl.CostEstimate(flops=2 * 10**9, bytes_accessed=10**7, transcendentals=0),
-        compiler_params=pltpu.CompilerParams(vmem_limit_bytes=36 * 2**20),
+        compiler_params=pltpu.CompilerParams(vmem_limit_bytes=28 * 2**20),
     )(place, own, neighbour)
-    mine, high = lax.optimization_barrier((mine, high))
     arrived = [from_group(mine, 2 * pair) for pair in range(1, size // 2)]
-    arrived[-1], early = lax.optimization_barrier((arrived[-1], early))
+    arrived[-1], early, high = lax.optimization_barrier((arrived[-1], early, high))
     operands = []
     for array in arrived:
         operands += [array, other_core(array)]
@@ -302,7 +296,7 @@
         functools.partial(image_kernel, smear_sizes, size, width, early_pitch, pitch, turn_pitch),
         name="image",
         out_shape=jax.ShapeDtypeStruct((turn_blocks * turned_rows, LANES), jnp.float32),
-        in_specs=[in_smem] + [in_vmem] * (size - 2) + [in_vmem] * 3,
+        in_specs=[in_smem] + [in_vmem] * (size - 2) + [in_vmem] * 4,
         out_specs=in_vmem,
         scratch_shapes=smear_scratch(size - 2)
         + [
@@ -310,8 +304,8 @@
             pltpu.SemaphoreType.DMA,
         ],
         cost_estimate=pl.CostEstimate(flops=10**10, bytes_accessed=10**7, transcendentals=0),
-        compiler_params=pltpu.CompilerParams(vmem_limit_bytes=40 * 2**20),
-    )(place, *operands, early, high, low)
+        compiler_params=pltpu.CompilerParams(vmem_limit_bytes=30 * 2**20),
+    )(place, *operands, early, shift, high, low)
     rows_spec = pl.BlockSpec((turned_rows, LANES), lambda i: (i, 0))
     block_rows = min(rows, LANES)
     return pl.pallas_call(

time: 59.4 us -> 56.7 us (0.955)
  Pallas kernels: 37.7 us -> 33.9 us
  waiting for transfers between devices: 8.77 us -> 9.86 us
    pallas_call x1, Pallas kernels: 23.6 us -> 21.4 us  [body(): pl.pallas_call(functools.partial(image_kernel, smear_sizes, size, width,...]
    ppermute x4, waiting for transfers between devices: 3.27 us -> 4.36 us  [from_group(): return lax.ppermute(array, 'ang', [(i, i ^ k) for i in range(size)])]
    pallas_call x1, Pallas kernels: 7.44 us -> 6.35 us  [body(): pl.pallas_call(functools.partial(early_kernel, smear_sizes, early_pitch),...]
  transfers between devices with their start and end apart: 8 -> 8, of which waited for: 5 -> 5; matrix products, arithmetic and copies ran while one was open for 0% -> 0% of each run, Pallas kernels for 17% -> 16%
where the time goes in v3:
time: 56.7 us; the launch traced here: 56.5 us
  Pallas kernels  33.9 us (60%)
  waiting for transfers between devices  9.86 us (17%)
  starting transfers between devices  8.26 us (15%)
  local copies, waits for them, and re-layouts  3.57 us (6%)
  other arithmetic  0.79 us (1%)
    pallas_call x1, Pallas kernels, body(): pl.pallas_call(functools.partial(image_kernel, smear_sizes, size, width,...  21.4 us
    ppermute x4, starting transfers between devices, from_group(): return lax.ppermute(array, 'ang', [(i, i ^ k) for i in range(size)])  7.48 us
    pallas_call x1, Pallas kernels, body(): pl.pallas_call(functools.partial(early_kernel, smear_sizes, early_pitch),...  6.35 us
    ppermute x4, waiting for transfers between devices, other_core(): return lax.ppermute(array, 'tile', [(i, i ^ 1) for i in range(tiles)])  5.5 us
    ppermute x4, waiting for transfers between devices, from_group(): return lax.ppermute(array, 'ang', [(i, i ^ k) for i in range(size)])  4.36 us
    pallas_call x1, Pallas kernels, body(): pl.pallas_call(functools.partial(finish_kernel, slices, run, turn_pitch),...  3.53 us
    pallas_call x1, Pallas kernels, body(): pl.pallas_call(functools.partial(matrices_kernel, levels, width, angles),...  2.61 us
    unnamed x3, local copies, waits for them, and re-layouts  1.9 us
  transfers between devices with their start and end apart: 8, of which 5 were waited for; matrix products, arithmetic and copies ran while one was open for 0% of the time, Pallas kernels for 16%

profile of v3, /device:TPU:0, one launch (start us, length us, event | category | flops | bytes accessed | tf_op | source)
XLA Modules:
  0.0 56.5 jit_solution(14787805971764577086)
XLA Ops:
  0.0 0.7 %convert_element_type.3 = f32[8,256]{1,0:T(8,128)S(1)} convert(s32[8,256]{1,0:T(8,128)} %param.4) | non-fusion elementwise | flops 2048 | bytes 16384 | tf_op jit(solution)/shard_map/convert_element_type | solution.py:22
  0.7 0.1 reshape.14
  0.8 0.1 reshape.15
  0.9 1.1 %reshape.12 = f32[2,2,4,64,32]{4,3,2,1,0:T(8,128)S(1)} reshape(f32[2,8,2048]{2,1,0:T(8,128)} %param.3) | data formatting | bytes 262144 | tf_op jit(solution)/shard_map/reshape | solution.py:20
  2.0 0.2 copy.6
  2.2 0.2 reshape.13
  2.4 3.0 %collective-permute-start = (f32[2,136,128]{2,1,0:T(8,128)S(1)}, f32[2,136,128]{2,1,0:T(8,128)S(1)}, u32[]{:S(2)}, u32[]{:S(2)}) collective-permute-start(f32[2,136,128]{2,1,0:T(8,128)S(1)} %constant_dynamic-update-slice_fusion.own_ref), channel_id=1, source_target_pairs={{0,4},{4,0},{8,12},{12,8},{16,20},{20,16},{24,28},{28,24},{1,5},{5... | collective-permute-start | bytes 417800 | tf_op jit(solution)/shard_map/ppermute | solution.py:236
  5.4 0.1 pad_add_fusion.place_ref
  5.5 0.0 copy-start
  5.5 1.9 %copy-done = f32[3,2,2,256,256]{4,3,2,1,0:T(8,128)S(1)} copy-done((f32[3,2,2,256,256]{4,3,2,1,0:T(8,128)S(1)}, f32[3,2,2,256,256]{4,3,2,1,0:T(8,128)}, u32[]{:S(2)}) %copy-start) | copy-done | bytes 3145752
  7.4 2.6 %matrices.1 = (bf16[256,1280]{1,0:T(8,128)(2,1)S(1)}, bf16[256,1280]{1,0:T(8,128)(2,1)S(1)}) custom-call(s32[3]{0:T(128)S(1)} %pad_add_fusion.place_ref, f32[3,2,2,256,256]{4,3,2,1,0:T(8,128)S(1)} %copy-done), custom_call_target="tpu_custom_call" | custom-call | flops 500000000 | bytes 1000000 | tf_op jit(solution)/shard_map/matrices/pallas_call | solution.py:264
  10.0 0.0 collective-permute-done.neighbour_ref
  10.1 3.7 %collective-permute-start.5 = (f32[2,136,128]{2,1,0:T(8,128)S(1)}, f32[2,136,128]{2,1,0:T(8,128)S(1)}, u32[]{:S(2)}, u32[]{:S(2)}) collective-permute-start(f32[2,136,128]{2,1,0:T(8,128)S(1)} %pad_maximum_fusion), channel_id=1, source_target_pairs={{0,24},{4,28},{8,16},{12,20},{16,8},{20,12},{24,0},{28,4},{1,25},{... | collective-permute-start | bytes 417800 | tf_op jit(solution)/shard_map/ppermute | solution.py:236
  13.7 0.0 collective-permute-start.3
  13.7 0.8 %collective-permute-start.1 = (f32[2,136,128]{2,1,0:T(8,128)S(1)}, f32[2,136,128]{2,1,0:T(8,128)S(1)}, u32[]{:S(2)}, u32[]{:S(2)}) collective-permute-start(f32[2,136,128]{2,1,0:T(8,128)S(1)} %pad_maximum_fusion), channel_id=1, source_target_pairs={{0,8},{4,12},{8,0},{12,4},{16,24},{20,28},{24,16},{28,20},{1,9},{5... | collective-permute-start | bytes 417800 | tf_op jit(solution)/shard_map/ppermute | solution.py:236
  14.5 6.3 %early.1 = (f32[5312,128]{1,0:T(8,128)S(1)}, bf16[256,8192]{1,0:T(8,128)(2,1)S(1)}) custom-call(s32[3]{0:T(128)S(1)} %pad_add_fusion.place_ref, f32[2,136,128]{2,1,0:T(8,128)S(1)} %constant_dynamic-update-slice_fusion.own_ref, f32[2,136,128]{2,1,0:T(8,128)S(1)} %collective-permute-done.neighbour_ref), custom_call_target="tpu_custom_call" | custom-call | flops 2000000000 | bytes 10000000 | tf_op jit(solution)/shard_map/early/pallas_call | solution.py:277
  20.9 0.0 collective-permute-done.5.refs_4_
  20.9 4.3 %collective-permute-done.3.refs_2_ = f32[2,136,128]{2,1,0:T(8,128)S(1)} collective-permute-done((f32[2,136,128]{2,1,0:T(8,128)S(1)}, f32[2,136,128]{2,1,0:T(8,128)S(1)}, u32[]{:S(2)}, u32[]{:S(2)}) %collective-permute-start.3) | collective-permute-done | bytes 139296 | tf_op jit(solution)/shard_map/ppermute | solution.py:236
  25.2 0.0 collective-permute-start.4
  25.2 0.0 collective-permute-done.1.refs_0_
  25.2 0.5 collective-permute-start.2
  25.8 0.0 collective-permute-start.6
  25.8 0.8 %collective-permute-done.4.refs_3_ = f32[2,136,128]{2,1,0:T(8,128)S(1)} collective-permute-done((f32[2,136,128]{2,1,0:T(8,128)S(1)}, f32[2,136,128]{2,1,0:T(8,128)S(1)}, u32[]{:S(2)}, u32[]{:S(2)}) %collective-permute-start.4) | collective-permute-done | bytes 139296 | tf_op jit(solution)/shard_map/ppermute | solution.py:233
  26.6 0.2 collective-permute-done.2.refs_1_
  26.8 0.3 collective-permute-done.6.refs_5_
  27.1 21.4 %image.1.own_ref = f32[4352,128]{1,0:T(8,128)S(1)} custom-call(s32[3]{0:T(128)S(1)} %pad_add_fusion.place_ref, f32[2,136,128]{2,1,0:T(8,128)S(1)} %collective-permute-done.1.refs_0_, f32[2,136,128]{2,1,0:T(8,128)S(1)} %collective-permute-done.2.refs_1_, f32[2,136,128]{2,1,0:T(8,128)S(1)} %collective-permute-done.3.refs_2_, ...), custom_call_target="tpu_custom_call" | custom-call | flops 10000000000 | bytes 10000000 | tf_op jit(solution)/shard_map/image/pallas_call | solution.py:295
  48.5 0.3 collective-permute-start.7
  48.8 4.1 %collective-permute-done.7.other_ref = f32[4352,128]{1,0:T(8,128)S(1)} collective-permute-done((f32[4352,128]{1,0:T(8,128)S(1)}, f32[4352,128]{1,0:T(8,128)S(1)}, u32[]{:S(2)}, u32[]{:S(2)}) %collective-permute-start.7) | collective-permute-done | bytes 2228256 | tf_op jit(solution)/shard_map/ppermute | solution.py:233
  53.0 3.5 %finish.1 = f32[2,256,2048]{2,1,0:T(8,128)} custom-call(s32[3]{0:T(128)S(1)} %pad_add_fusion.place_ref, f32[4352,128]{1,0:T(8,128)S(1)} %image.1.own_ref, f32[4352,128]{1,0:T(8,128)S(1)} %collective-permute-done.7.other_ref), custom_call_target="tpu_custom_call" | custom-call | flops 100000000 | bytes 10000000 | tf_op jit(solution)/shard_map/finish/pallas_call | solution.py:311
  (6 shorter events, 0.1 us)
Async XLA Ops:
  2.4 7.6 %collective-permute-start = (f32[2,136,128]{2,1,0:T(8,128)S(1)}, f32[2,136,128]{2,1,0:T(8,128)S(1)}, u32[]{:S(2)}, u32[]{:S(2)}) collective-permute-start(f32[2,136,128]{2,1,0:T(8,128)S(1)} %constant_dynamic-update-slice_fusion.own_ref), channel_id=1, source_target_pairs={{0,4},{4,0},{8,12},{12,8},{16,20},{20,16},{24,28},{28,24},{1,5},{5... | collective-permute-start | bytes 417800 | tf_op jit(solution)/shard_map/ppermute | solution.py:236
  5.5 1.9 %copy-start = (f32[3,2,2,256,256]{4,3,2,1,0:T(8,128)S(1)}, f32[3,2,2,256,256]{4,3,2,1,0:T(8,128)}, u32[]{:S(2)}) copy-start(f32[3,2,2,256,256]{4,3,2,1,0:T(8,128)} %all_ref.1) | copy-start | bytes 9437188
  10.1 10.8 %collective-permute-start.5 = (f32[2,136,128]{2,1,0:T(8,128)S(1)}, f32[2,136,128]{2,1,0:T(8,128)S(1)}, u32[]{:S(2)}, u32[]{:S(2)}) collective-permute-start(f32[2,136,128]{2,1,0:T(8,128)S(1)} %pad_maximum_fusion), channel_id=1, source_target_pairs={{0,24},{4,28},{8,16},{12,20},{16,8},{20,12},{24,0},{28,4},{1,25},{... | collective-permute-start | bytes 417800 | tf_op jit(solution)/shard_map/ppermute | solution.py:236
  13.7 11.5 %collective-permute-start.3 = (f32[2,136,128]{2,1,0:T(8,128)S(1)}, f32[2,136,128]{2,1,0:T(8,128)S(1)}, u32[]{:S(2)}, u32[]{:S(2)}) collective-permute-start(f32[2,136,128]{2,1,0:T(8,128)S(1)} %pad_maximum_fusion), channel_id=1, source_target_pairs={{0,16},{4,20},{8,24},{12,28},{16,0},{20,4},{24,8},{28,12},{1,17},{... | collective-permute-start | bytes 417800 | tf_op jit(solution)/shard_map/ppermute | solution.py:236
  13.7 11.5 %collective-permute-start.1 = (f32[2,136,128]{2,1,0:T(8,128)S(1)}, f32[2,136,128]{2,1,0:T(8,128)S(1)}, u32[]{:S(2)}, u32[]{:S(2)}) collective-permute-start(f32[2,136,128]{2,1,0:T(8,128)S(1)} %pad_maximum_fusion), channel_id=1, source_target_pairs={{0,8},{4,12},{8,0},{12,4},{16,24},{20,28},{24,16},{28,20},{1,9},{5... | collective-permute-start | bytes 417800 | tf_op jit(solution)/shard_map/ppermute | solution.py:236
  25.2 1.4 %collective-permute-start.4 = (f32[2,136,128]{2,1,0:T(8,128)S(1)}, f32[2,136,128]{2,1,0:T(8,128)S(1)}, u32[]{:S(2)}, u32[]{:S(2)}) collective-permute-start(f32[2,136,128]{2,1,0:T(8,128)S(1)} %collective-permute-done.3.refs_2_), channel_id=1, source_target_pairs={{0,1},{1,0},{2,3},{3,2},{4,5},{5,4},{6,7},{7,6},{8,9},{9,8},{10,11... | collective-permute-start | bytes 417800 | tf_op jit(solution)/shard_map/ppermute | solution.py:233
  25.2 1.6 %collective-permute-start.2 = (f32[2,136,128]{2,1,0:T(8,128)S(1)}, f32[2,136,128]{2,1,0:T(8,128)S(1)}, u32[]{:S(2)}, u32[]{:S(2)}) collective-permute-start(f32[2,136,128]{2,1,0:T(8,128)S(1)} %collective-permute-done.1.refs_0_), channel_id=1, source_target_pairs={{0,1},{1,0},{2,3},{3,2},{4,5},{5,4},{6,7},{7,6},{8,9},{9,8},{10,11... | collective-permute-start | bytes 417800 | tf_op jit(solution)/shard_map/ppermute | solution.py:233
  25.8 1.4 %collective-permute-start.6 = (f32[2,136,128]{2,1,0:T(8,128)S(1)}, f32[2,136,128]{2,1,0:T(8,128)S(1)}, u32[]{:S(2)}, u32[]{:S(2)}) collective-permute-start(f32[2,136,128]{2,1,0:T(8,128)S(1)} %collective-permute-done.5.refs_4_), channel_id=1, source_target_pairs={{0,1},{1,0},{2,3},{3,2},{4,5},{5,4},{6,7},{7,6},{8,9},{9,8},{10,11... | collective-permute-start | bytes 417800 | tf_op jit(solution)/shard_map/ppermute | solution.py:233
  48.5 4.4 %collective-permute-start.7 = (f32[4352,128]{1,0:T(8,128)S(1)}, f32[4352,128]{1,0:T(8,128)S(1)}, u32[]{:S(2)}, u32[]{:S(2)}) collective-permute-start(f32[4352,128]{1,0:T(8,128)S(1)} %image.1.own_ref), channel_id=1, source_target_pairs={{0,1},{1,0},{2,3},{3,2},{4,5},{5,4},{6,7},{7,6},{8,9},{9,8},{10,11... | collective-permute-start | bytes 6684680 | tf_op jit(solution)/shard_map/ppermute | solution.py:233

commit v4 on v3

--- a/solution.py
+++ b/solution.py
@@ -192,7 +192,7 @@
                 out_ref[pl.ds(start, LANES, stride=turn_pitch), :part] = turned[:, r : r + part]
         return carry
 
-    lax.fori_loop(0, run // 4, multiply_block, 0, unroll=4)
+    lax.fori_loop(0, run // 4, multiply_block, 0, unroll=8)
 
 
 def finish_kernel(slices, run, turn_pitch, place_ref, own_ref, other_ref, out_ref):
@@ -212,7 +212,7 @@
             out_ref[s, :, columns] = jnp.concatenate(pieces, axis=0).T[:part]
         return carry
 
-    lax.fori_loop(0, lane_blocks // per, turn_block, 0, unroll=4)
+    lax.fori_loop(0, lane_blocks // per, turn_block, 0, unroll=8)
 
 
 def body(sinogram, ray_offsets, merge_matrices):

time: 56.7 us -> 56.1 us (0.989)
  Pallas kernels: 33.9 us -> 33.3 us
where the time goes in v4:
time: 56.1 us; the launch traced here: 55.9 us
  Pallas kernels  33.3 us (59%)
  waiting for transfers between devices  9.86 us (18%)
  starting transfers between devices  8.26 us (15%)
  local copies, waits for them, and re-layouts  3.57 us (6%)
  other arithmetic  0.79 us (1%)
    pallas_call x1, Pallas kernels, body(): pl.pallas_call(functools.partial(image_kernel, smear_sizes, size, width,...  21.1 us
    ppermute x4, starting transfers between devices, from_group(): return lax.ppermute(array, 'ang', [(i, i ^ k) for i in range(size)])  7.48 us
    pallas_call x1, Pallas kernels, body(): pl.pallas_call(functools.partial(early_kernel, smear_sizes, early_pitch),...  6.35 us
    ppermute x4, waiting for transfers between devices, other_core(): return lax.ppermute(array, 'tile', [(i, i ^ 1) for i in range(tiles)])  5.5 us
    ppermute x4, waiting for transfers between devices, from_group(): return lax.ppermute(array, 'ang', [(i, i ^ k) for i in range(size)])  4.36 us
    pallas_call x1, Pallas kernels, body(): pl.pallas_call(functools.partial(finish_kernel, slices, run, turn_pitch),...  3.25 us
    pallas_call x1, Pallas kernels, body(): pl.pallas_call(functools.partial(matrices_kernel, levels, width, angles),...  2.61 us
    unnamed x3, local copies, waits for them, and re-layouts  1.9 us
  transfers between devices with their start and end apart: 8, of which 5 were waited for; matrix products, arithmetic and copies ran while one was open for 0% of the time, Pallas kernels for 16%

profile of v4, /device:TPU:0, one launch (start us, length us, event | category | flops | bytes accessed | tf_op | source)
XLA Modules:
  0.0 55.9 jit_solution(14626514558834021737)
XLA Ops:
  0.0 0.7 %convert_element_type.3 = f32[8,256]{1,0:T(8,128)S(1)} convert(s32[8,256]{1,0:T(8,128)} %param.4) | non-fusion elementwise | flops 2048 | bytes 16384 | tf_op jit(solution)/shard_map/convert_element_type | solution.py:22
  0.7 0.1 reshape.14
  0.8 0.1 reshape.15
  0.9 1.1 %reshape.12 = f32[2,2,4,64,32]{4,3,2,1,0:T(8,128)S(1)} reshape(f32[2,8,2048]{2,1,0:T(8,128)} %param.3) | data formatting | bytes 262144 | tf_op jit(solution)/shard_map/reshape | solution.py:20
  2.0 0.2 copy.6
  2.2 0.2 reshape.13
  2.4 3.0 %collective-permute-start = (f32[2,136,128]{2,1,0:T(8,128)S(1)}, f32[2,136,128]{2,1,0:T(8,128)S(1)}, u32[]{:S(2)}, u32[]{:S(2)}) collective-permute-start(f32[2,136,128]{2,1,0:T(8,128)S(1)} %constant_dynamic-update-slice_fusion.own_ref), channel_id=1, source_target_pairs={{0,4},{4,0},{8,12},{12,8},{16,20},{20,16},{24,28},{28,24},{1,5},{5... | collective-permute-start | bytes 417800 | tf_op jit(solution)/shard_map/ppermute | solution.py:236
  5.4 0.1 pad_add_fusion.place_ref
  5.5 0.0 copy-start
  5.5 1.9 %copy-done = f32[3,2,2,256,256]{4,3,2,1,0:T(8,128)S(1)} copy-done((f32[3,2,2,256,256]{4,3,2,1,0:T(8,128)S(1)}, f32[3,2,2,256,256]{4,3,2,1,0:T(8,128)}, u32[]{:S(2)}) %copy-start) | copy-done | bytes 3145752
  7.4 2.6 %matrices.1 = (bf16[256,1280]{1,0:T(8,128)(2,1)S(1)}, bf16[256,1280]{1,0:T(8,128)(2,1)S(1)}) custom-call(s32[3]{0:T(128)S(1)} %pad_add_fusion.place_ref, f32[3,2,2,256,256]{4,3,2,1,0:T(8,128)S(1)} %copy-done), custom_call_target="tpu_custom_call" | custom-call | flops 500000000 | bytes 1000000 | tf_op jit(solution)/shard_map/matrices/pallas_call | solution.py:264
  10.0 0.0 collective-permute-done.neighbour_ref
  10.1 3.7 %collective-permute-start.5 = (f32[2,136,128]{2,1,0:T(8,128)S(1)}, f32[2,136,128]{2,1,0:T(8,128)S(1)}, u32[]{:S(2)}, u32[]{:S(2)}) collective-permute-start(f32[2,136,128]{2,1,0:T(8,128)S(1)} %pad_maximum_fusion), channel_id=1, source_target_pairs={{0,24},{4,28},{8,16},{12,20},{16,8},{20,12},{24,0},{28,4},{1,25},{... | collective-permute-start | bytes 417800 | tf_op jit(solution)/shard_map/ppermute | solution.py:236
  13.7 0.0 collective-permute-start.3
  13.7 0.8 %collective-permute-start.1 = (f32[2,136,128]{2,1,0:T(8,128)S(1)}, f32[2,136,128]{2,1,0:T(8,128)S(1)}, u32[]{:S(2)}, u32[]{:S(2)}) collective-permute-start(f32[2,136,128]{2,1,0:T(8,128)S(1)} %pad_maximum_fusion), channel_id=1, source_target_pairs={{0,8},{4,12},{8,0},{12,4},{16,24},{20,28},{24,16},{28,20},{1,9},{5... | collective-permute-start | bytes 417800 | tf_op jit(solution)/shard_map/ppermute | solution.py:236
  14.5 6.3 %early.1 = (f32[5312,128]{1,0:T(8,128)S(1)}, bf16[256,8192]{1,0:T(8,128)(2,1)S(1)}) custom-call(s32[3]{0:T(128)S(1)} %pad_add_fusion.place_ref, f32[2,136,128]{2,1,0:T(8,128)S(1)} %constant_dynamic-update-slice_fusion.own_ref, f32[2,136,128]{2,1,0:T(8,128)S(1)} %collective-permute-done.neighbour_ref), custom_call_target="tpu_custom_call" | custom-call | flops 2000000000 | bytes 10000000 | tf_op jit(solution)/shard_map/early/pallas_call | solution.py:277
  20.9 0.0 collective-permute-done.5.refs_4_
  20.9 4.3 %collective-permute-done.3.refs_2_ = f32[2,136,128]{2,1,0:T(8,128)S(1)} collective-permute-done((f32[2,136,128]{2,1,0:T(8,128)S(1)}, f32[2,136,128]{2,1,0:T(8,128)S(1)}, u32[]{:S(2)}, u32[]{:S(2)}) %collective-permute-start.3) | collective-permute-done | bytes 139296 | tf_op jit(solution)/shard_map/ppermute | solution.py:236
  25.2 0.0 collective-permute-start.4
  25.2 0.0 collective-permute-done.1.refs_0_
  25.2 0.5 collective-permute-start.2
  25.8 0.0 collective-permute-start.6
  25.8 0.8 %collective-permute-done.4.refs_3_ = f32[2,136,128]{2,1,0:T(8,128)S(1)} collective-permute-done((f32[2,136,128]{2,1,0:T(8,128)S(1)}, f32[2,136,128]{2,1,0:T(8,128)S(1)}, u32[]{:S(2)}, u32[]{:S(2)}) %collective-permute-start.4) | collective-permute-done | bytes 139296 | tf_op jit(solution)/shard_map/ppermute | solution.py:233
  26.6 0.2 collective-permute-done.2.refs_1_
  26.8 0.3 collective-permute-done.6.refs_5_
  27.1 21.1 %image.1.own_ref = f32[4352,128]{1,0:T(8,128)S(1)} custom-call(s32[3]{0:T(128)S(1)} %pad_add_fusion.place_ref, f32[2,136,128]{2,1,0:T(8,128)S(1)} %collective-permute-done.1.refs_0_, f32[2,136,128]{2,1,0:T(8,128)S(1)} %collective-permute-done.2.refs_1_, f32[2,136,128]{2,1,0:T(8,128)S(1)} %collective-permute-done.3.refs_2_, ...), custom_call_target="tpu_custom_call" | custom-call | flops 10000000000 | bytes 10000000 | tf_op jit(solution)/shard_map/image/pallas_call | solution.py:295
  48.2 0.3 collective-permute-start.7
  48.5 4.1 %collective-permute-done.7.other_ref = f32[4352,128]{1,0:T(8,128)S(1)} collective-permute-done((f32[4352,128]{1,0:T(8,128)S(1)}, f32[4352,128]{1,0:T(8,128)S(1)}, u32[]{:S(2)}, u32[]{:S(2)}) %collective-permute-start.7) | collective-permute-done | bytes 2228256 | tf_op jit(solution)/shard_map/ppermute | solution.py:233
  52.6 3.2 %finish.1 = f32[2,256,2048]{2,1,0:T(8,128)} custom-call(s32[3]{0:T(128)S(1)} %pad_add_fusion.place_ref, f32[4352,128]{1,0:T(8,128)S(1)} %image.1.own_ref, f32[4352,128]{1,0:T(8,128)S(1)} %collective-permute-done.7.other_ref), custom_call_target="tpu_custom_call" | custom-call | flops 100000000 | bytes 10000000 | tf_op jit(solution)/shard_map/finish/pallas_call | solution.py:311
  (6 shorter events, 0.1 us)
Async XLA Ops:
  2.4 7.6 %collective-permute-start = (f32[2,136,128]{2,1,0:T(8,128)S(1)}, f32[2,136,128]{2,1,0:T(8,128)S(1)}, u32[]{:S(2)}, u32[]{:S(2)}) collective-permute-start(f32[2,136,128]{2,1,0:T(8,128)S(1)} %constant_dynamic-update-slice_fusion.own_ref), channel_id=1, source_target_pairs={{0,4},{4,0},{8,12},{12,8},{16,20},{20,16},{24,28},{28,24},{1,5},{5... | collective-permute-start | bytes 417800 | tf_op jit(solution)/shard_map/ppermute | solution.py:236
  5.5 1.9 %copy-start = (f32[3,2,2,256,256]{4,3,2,1,0:T(8,128)S(1)}, f32[3,2,2,256,256]{4,3,2,1,0:T(8,128)}, u32[]{:S(2)}) copy-start(f32[3,2,2,256,256]{4,3,2,1,0:T(8,128)} %all_ref.1) | copy-start | bytes 9437188
  10.1 10.8 %collective-permute-start.5 = (f32[2,136,128]{2,1,0:T(8,128)S(1)}, f32[2,136,128]{2,1,0:T(8,128)S(1)}, u32[]{:S(2)}, u32[]{:S(2)}) collective-permute-start(f32[2,136,128]{2,1,0:T(8,128)S(1)} %pad_maximum_fusion), channel_id=1, source_target_pairs={{0,24},{4,28},{8,16},{12,20},{16,8},{20,12},{24,0},{28,4},{1,25},{... | collective-permute-start | bytes 417800 | tf_op jit(solution)/shard_map/ppermute | solution.py:236
  13.7 11.5 %collective-permute-start.3 = (f32[2,136,128]{2,1,0:T(8,128)S(1)}, f32[2,136,128]{2,1,0:T(8,128)S(1)}, u32[]{:S(2)}, u32[]{:S(2)}) collective-permute-start(f32[2,136,128]{2,1,0:T(8,128)S(1)} %pad_maximum_fusion), channel_id=1, source_target_pairs={{0,16},{4,20},{8,24},{12,28},{16,0},{20,4},{24,8},{28,12},{1,17},{... | collective-permute-start | bytes 417800 | tf_op jit(solution)/shard_map/ppermute | solution.py:236
  13.7 11.5 %collective-permute-start.1 = (f32[2,136,128]{2,1,0:T(8,128)S(1)}, f32[2,136,128]{2,1,0:T(8,128)S(1)}, u32[]{:S(2)}, u32[]{:S(2)}) collective-permute-start(f32[2,136,128]{2,1,0:T(8,128)S(1)} %pad_maximum_fusion), channel_id=1, source_target_pairs={{0,8},{4,12},{8,0},{12,4},{16,24},{20,28},{24,16},{28,20},{1,9},{5... | collective-permute-start | bytes 417800 | tf_op jit(solution)/shard_map/ppermute | solution.py:236
  25.2 1.4 %collective-permute-start.4 = (f32[2,136,128]{2,1,0:T(8,128)S(1)}, f32[2,136,128]{2,1,0:T(8,128)S(1)}, u32[]{:S(2)}, u32[]{:S(2)}) collective-permute-start(f32[2,136,128]{2,1,0:T(8,128)S(1)} %collective-permute-done.3.refs_2_), channel_id=1, source_target_pairs={{0,1},{1,0},{2,3},{3,2},{4,5},{5,4},{6,7},{7,6},{8,9},{9,8},{10,11... | collective-permute-start | bytes 417800 | tf_op jit(solution)/shard_map/ppermute | solution.py:233
  25.2 1.6 %collective-permute-start.2 = (f32[2,136,128]{2,1,0:T(8,128)S(1)}, f32[2,136,128]{2,1,0:T(8,128)S(1)}, u32[]{:S(2)}, u32[]{:S(2)}) collective-permute-start(f32[2,136,128]{2,1,0:T(8,128)S(1)} %collective-permute-done.1.refs_0_), channel_id=1, source_target_pairs={{0,1},{1,0},{2,3},{3,2},{4,5},{5,4},{6,7},{7,6},{8,9},{9,8},{10,11... | collective-permute-start | bytes 417800 | tf_op jit(solution)/shard_map/ppermute | solution.py:233
  25.8 1.4 %collective-permute-start.6 = (f32[2,136,128]{2,1,0:T(8,128)S(1)}, f32[2,136,128]{2,1,0:T(8,128)S(1)}, u32[]{:S(2)}, u32[]{:S(2)}) collective-permute-start(f32[2,136,128]{2,1,0:T(8,128)S(1)} %collective-permute-done.5.refs_4_), channel_id=1, source_target_pairs={{0,1},{1,0},{2,3},{3,2},{4,5},{5,4},{6,7},{7,6},{8,9},{9,8},{10,11... | collective-permute-start | bytes 417800 | tf_op jit(solution)/shard_map/ppermute | solution.py:233
  48.2 4.4 %collective-permute-start.7 = (f32[4352,128]{1,0:T(8,128)S(1)}, f32[4352,128]{1,0:T(8,128)S(1)}, u32[]{:S(2)}, u32[]{:S(2)}) collective-permute-start(f32[4352,128]{1,0:T(8,128)S(1)} %image.1.own_ref), channel_id=1, source_target_pairs={{0,1},{1,0},{2,3},{3,2},{4,5},{5,4},{6,7},{7,6},{8,9},{9,8},{10,11... | collective-permute-start | bytes 6684680 | tf_op jit(solution)/shard_map/ppermute | solution.py:233
